TPU v7x, 32 devices: a whole 2x2x4 slice. The times are simulated.
32 devices in a mesh: expert: 4 (over y, x), tensor: 4 (over z), replica: 2 (over core).
Axes of the slice: x: 2, y: 2, z: 4, core: 2. Of those that a mesh axis runs over, the one named last changes fastest.
Arguments:
- trained: float32 [4, 7168, 2048], P('replica', 'tensor', 'expert'), may hold values from -3080 to 3080
- snapshot: bfloat16 [4, 7168, 2048], P('replica', 'tensor', 'expert'), may hold values from -3072 to 3072
- changed: int32 [4, 56, 16], P('replica', 'tensor', 'expert'), may hold values from 0 to 1, as said below
- placement: int32 [4], replicated, may hold values from 0 to 3, each once
Outputs:
- rotated_update: bfloat16 [4, 7168, 2048], P('expert', None, 'tensor')
Inputs may be any that keep to these rules, and one draw needn't show every extreme that they name: `placement`: each of the 4 experts appears exactly once. `changed`: in each aligned block of 14 block rows by 4 block columns of one expert, at most 32 entries are 1; for every expert some such block has exactly 32.
All inputs are finite; a program needn't handle non-finite values.
Results may differ from a plain program's by a relative error of at most 0.001.
Values may be sent and summed in bfloat16 or wider, within the bound.
No kernel may reach another device: no remote copies, remote signals or barrier semaphores. Data moves between devices by JAX's collectives and lax.ppermute only.
A program may use at most 64 MiB of HBM per device.

v0:
```python
import math

import jax
import jax.numpy as jnp
from jax import lax
from jax.sharding import PartitionSpec as P

BLK = 128


def hadamard():
    positions = jnp.arange(BLK, dtype=jnp.int32)
    parity = jnp.zeros((BLK, BLK), jnp.int32)
    for bit_level in range(BLK.bit_length() - 1):
        parity = parity + (positions[:, None] >> bit_level & 1) * (
            positions[None, :] >> bit_level & 1
        )
    return (1 - 2 * (parity % 2)).astype(jnp.float32) / math.sqrt(BLK)


def body(trained, snapshot, changed, placement):
    hadamard_table = hadamard()
    local_experts, local_rows, local_cols = trained.shape
    copies = lax.axis_size("replica")
    tensor_count = lax.axis_size("tensor")
    expert_count = lax.axis_size("expert")
    members = expert_count // tensor_count
    slot_total = placement.shape[0]
    owner_slots = slot_total // expert_count
    block_rows = local_rows // BLK
    block_cols = local_cols // BLK
    part_rows = BLK // copies
    block_count = block_rows * block_cols
    capacity = (4 * block_count + 3) // 7
    block_flags = changed.reshape(local_experts, block_count)
    position = jnp.arange(block_count, dtype=jnp.int32)
    ranking = jnp.where(block_flags == 1, position[None, :], block_count + position[None, :])
    picked = jnp.argsort(ranking, axis=1)[:, :capacity]
    used_slots = jnp.take_along_axis(block_flags, picked, axis=1)
    expert_ids = jnp.arange(local_experts, dtype=jnp.int32)[:, None]
    row_ids = picked // block_cols
    col_ids = picked % block_cols
    new_tiles = trained.reshape(local_experts, block_rows, BLK, block_cols, BLK)[
        expert_ids, row_ids, :, col_ids, :
    ]
    old_tiles = snapshot.reshape(local_experts, block_rows, BLK, block_cols, BLK)[
        expert_ids, row_ids, :, col_ids, :
    ]
    delta_tiles = jnp.where(
        used_slots[:, :, None, None] == 1, new_tiles - old_tiles.astype(jnp.float32), 0.0
    )
    coded_tiles = jnp.einsum(
        "ij,pmjk->pmik", hadamard_table, delta_tiles, precision=lax.Precision.HIGHEST
    ).astype(jnp.bfloat16)
    coded_tiles = coded_tiles.reshape(local_experts, capacity, copies, part_rows, BLK)
    spots_pair = jnp.broadcast_to(picked[:, :, None], (local_experts, capacity, copies))
    tiles_all, spots_all = (
        lax.all_to_all(coded_tiles, "replica", split_axis=2, concat_axis=0, tiled=True),
        lax.all_to_all(spots_pair, "replica", split_axis=2, concat_axis=0, tiled=True),
    )
    chosen = jnp.take(tiles_all, placement, axis=0).reshape(
        slot_total, 1, 1, capacity, part_rows, BLK
    )
    chosen_spots = jnp.take(spots_all, placement, axis=0).reshape(slot_total, 1, 1, capacity)
    tiles_in, spot_numbers = (
        lax.all_to_all(
            lax.all_to_all(chosen, "expert", split_axis=0, concat_axis=2, tiled=True),
            "tensor",
            split_axis=2,
            concat_axis=1,
            tiled=True,
        ),
        lax.all_to_all(
            lax.all_to_all(chosen_spots, "expert", split_axis=0, concat_axis=2, tiled=True),
            "tensor",
            split_axis=2,
            concat_axis=1,
            tiled=True,
        ),
    )
    source_count = tiles_in.shape[1]
    one_hot = (spot_numbers[..., None] == position).astype(jnp.bfloat16)
    placed = jnp.einsum(
        "osnmg,osnmab->osngab", one_hot, tiles_in, preferred_element_type=jnp.float32
    ).astype(jnp.bfloat16)
    placed = placed.reshape(
        owner_slots, source_count, members, block_rows, block_cols, part_rows, BLK
    )
    placed = jnp.transpose(placed, (0, 1, 3, 5, 2, 4, 6))
    owner_cols = members * block_cols * BLK
    owned_rows = placed.reshape(owner_slots, source_count, block_rows, 1, part_rows, owner_cols)
    whole_rows = lax.all_gather(owned_rows, "replica", axis=3, tiled=True)
    return whole_rows.reshape(owner_slots, tensor_count * block_rows * BLK, owner_cols)


def solution(mesh):
    in_specs = (
        P("replica", "tensor", "expert"),
        P("replica", "tensor", "expert"),
        P("replica", "tensor", "expert"),
        P(),
    )
    out_specs = P("expert", None, "tensor")
    return jax.shard_map(body, mesh=mesh, in_specs=in_specs, out_specs=out_specs, check_vma=False)
```

profile of v0, /device:TPU:0, one launch (start us, length us, event | category | flops | bytes accessed | tf_op | source)
XLA Modules:
  0.0 204.7 jit_solution(14261060630009200218)
XLA Ops:
  6.5 0.8 copy.56
  7.6 1.0 sort.17
  9.3 3.2 %all-to-all-start = ((s32[2,32,2]{1,0,2:T(2,128)}), s32[2,32,2]{1,0,2:T(2,128)S(1)}, u32[]{:S(2)}, u32[]{:S(2)}) async-start(s32[2,32,2]{1,0,2:T(2,128)} %broadcast_in_dim.62), calls=%async_computation | async-start | bytes 4096 | tf_op jit(solution)/shard_map/all_to_all | solution.py:59
  12.6 0.7 compare_select_fusion.2
  13.2 0.7 compare_and_fusion
  13.9 9.5 %reshape.222 = f32[2,14,128,4,128]{4,3,2,1,0:T(4,128)} reshape(f32[2,1792,512]{2,1,0:T(8,128)} %param.4) | data formatting | bytes 14680064 | tf_op jit(solution)/shard_map/reshape | solution.py:43
  23.4 7.1 %copy.63 = f32[2,14,128,4,128]{4,2,3,1,0:T(8,128)} copy(f32[2,14,128,4,128]{4,3,2,1,0:T(4,128)} %reshape.222) | data formatting | bytes 14680064 | tf_op jit(solution)/shard_map/reshape | solution.py:43
  30.6 6.3 %reshape.223 = bf16[2,14,128,4,128]{4,3,2,1,0:T(4,128)(2,1)} reshape(bf16[2,1792,512]{2,1,0:T(8,128)(2,1)} %param.5) | data formatting | bytes 7340032 | tf_op jit(solution)/shard_map/reshape | solution.py:46
  36.9 5.0 %copy.64 = bf16[2,14,128,4,128]{4,2,3,1,0:T(8,128)(2,1)} copy(bf16[2,14,128,4,128]{4,3,2,1,0:T(4,128)(2,1)} %reshape.223) | data formatting | bytes 7340032 | tf_op jit(solution)/shard_map/reshape | solution.py:46
  41.9 5.9 %gather_fusion.1 = f32[64,128,128]{2,1,0:T(8,128)} fusion(f32[2,14,128,4,128]{4,2,3,1,0:T(8,128)} %copy.63, s32[64]{0:T(128)S(1)} %reshape.239), kind=kCustom, calls=%fused_computation.1 | custom fusion | bytes 8389376 | tf_op jit(solution)/shard_map/gather | solution.py:43
  47.8 3.1 %gather_fusion.2 = bf16[64,128,128]{2,1,0:T(8,128)(2,1)S(1)} fusion(bf16[2,14,128,4,128]{4,2,3,1,0:T(8,128)(2,1)} %copy.64, s32[64]{0:T(128)S(1)} %reshape.239), kind=kCustom, calls=%fused_computation.2 | custom fusion | bytes 4195072 | tf_op jit(solution)/shard_map/gather | solution.py:46
  50.9 0.9 gather_fusion.4
  51.9 2.9 %convert_subtract_fusion = f32[64,128,128]{2,1,0:T(8,128)S(1)} fusion(f32[64,128,128]{2,1,0:T(8,128)} %gather_fusion.1, bf16[64,128,128]{2,1,0:T(8,128)(2,1)S(1)} %gather_fusion.2), kind=kLoop, calls=%fused_computation.5 | loop fusion | flops 2097152 | bytes 10485760 | tf_op jit(solution)/shard_map/sub | solution.py:50
  54.8 4.6 %fusion.5 = bf16[2,32,128,128]{2,3,1,0:T(8,128)(2,1)S(1)} fusion(f32[2,32,128,128]{3,2,1,0:T(8,128)S(1)} %bitcast.63, pred[2,32]{1,0:T(4,128)(4,1)S(1)} %fusion.44, s32[128]{0:T(128)S(1)} %get-tuple-element.9, s32[128]{0:T(128)S(1)} %get-tuple-element.10, s32[128]{0:T(128)S(1)} %get-tuple-element.11, s32[128]{0:T(128)S(1)} %get-tuple-element.12, ...), kind=kOutput, calls=%fused_computation.14 | convolution fusion | flops 1613168640 | bytes 6295104 | tf_op jit(solution)/shard_map/ij,pmjk->pmik/dot_general | solution.py:52
  59.4 1.5 copy.65
  60.9 3.8 %all-to-all-start.3 = ((bf16[2,32,2,64,128]{4,3,1,0,2:T(8,128)(2,1)}), bf16[2,32,2,64,128]{4,3,1,0,2:T(8,128)(2,1)S(1)}, u32[]{:S(2)}, u32[]{:S(2)}) async-start(bf16[2,32,2,64,128]{4,3,1,0,2:T(8,128)(2,1)} %copy.65), calls=%async_computation.3 | async-start | bytes 4194304 | tf_op jit(solution)/shard_map/all_to_all | solution.py:58
  65.3 0.7 bitcast_select_fusion.1
  65.9 1.6 all-to-all-done.3
  67.5 5.2 %all-to-all-start.1 = ((s32[4,1,1,32]{3,2,1,0:T(1,128)}), s32[4,1,1,32]{3,2,1,0:T(1,128)}, u32[]{:S(2)}, u32[]{:S(2)}) async-start(s32[4,1,1,32]{3,2,1,0:T(1,128)} %bitcast.4), calls=%async_computation.1 | async-start | bytes 4096 | tf_op jit(solution)/shard_map/all_to_all | solution.py:74
  72.7 2.1 %gather_fusion.3 = bf16[4,32,64,128]{3,2,1,0:T(8,128)(2,1)} fusion(bf16[4,32,64,128]{3,2,1,0:T(8,128)(2,1)S(1)} %bitcast.67, s32[1024]{0:T(1024)S(1)} %pad_clamp_fusion), kind=kCustom, calls=%fused_computation.3 | custom fusion | bytes 4194320 | tf_op jit(solution)/shard_map/jit(_take)/gather | solution.py:61
  74.9 2.5 %all-to-all-done.1 = s32[4,1,1,32]{3,2,1,0:T(1,128)} async-done(((s32[4,1,1,32]{3,2,1,0:T(1,128)}), s32[4,1,1,32]{3,2,1,0:T(1,128)}, u32[]{:S(2)}, u32[]{:S(2)}) %all-to-all-start.1) | async-done | bytes 544 | tf_op jit(solution)/shard_map/all_to_all | solution.py:74
  77.4 4.9 %all-to-all-start.2 = ((s32[1,1,4,32]{3,1,0,2:T(1,128)}), s32[1,1,4,32]{3,1,0,2:T(1,128)S(1)}, u32[]{:S(2)}, u32[]{:S(2)}) async-start(s32[1,1,4,32]{3,1,0,2:T(1,128)} %bitcast.6), calls=%async_computation.2 | async-start | bytes 4096 | tf_op jit(solution)/shard_map/all_to_all | solution.py:73
  82.2 1.9 bitcast_select_fusion
  84.1 1.4 copy.66
  85.4 2.4 %all-to-all-done.2 = s32[1,1,4,32]{3,1,0,2:T(1,128)S(1)} async-done(((s32[1,1,4,32]{3,1,0,2:T(1,128)}), s32[1,1,4,32]{3,1,0,2:T(1,128)S(1)}, u32[]{:S(2)}, u32[]{:S(2)}) %all-to-all-start.2) | async-done | bytes 544 | tf_op jit(solution)/shard_map/all_to_all | solution.py:73
  87.8 25.7 %all_to_all.78 = bf16[4,1,1,32,64,128]{5,3,4,2,1,0:T(8,128)(2,1)S(1)} all-to-all(bf16[4,1,1,32,64,128]{5,3,4,2,1,0:T(8,128)(2,1)S(1)} %copy.66), channel_id=1, replica_groups=mesh['expert'=4,'tensor'=4,'replica'=2] {'expert'}, dimensions={0} | all-to-all | bytes 4194304 | tf_op jit(solution)/shard_map/all_to_all | solution.py:67
  113.5 48.9 %all_to_all.79 = bf16[1,1,4,32,64,128]{5,3,4,1,0,2:T(8,128)(2,1)S(1)} all-to-all(bf16[1,1,4,32,64,128]{5,3,4,1,0,2:T(8,128)(2,1)S(1)} %bitcast.68), channel_id=1, replica_groups=mesh['expert'=4,'tensor'=4,'replica'=2] {'tensor'}, dimensions={2} | all-to-all | bytes 4194304 | tf_op jit(solution)/shard_map/all_to_all | solution.py:66
  162.4 1.2 convolution_convert_fusion
  163.7 3.9 %copy.75 = bf16[1,4,1,14,4,64,128]{6,4,5,3,1,2,0:T(4,128)(2,1)} copy(bf16[1,4,1,14,4,64,128]{6,4,3,5,1,2,0:T(4,128)(2,1)S(1)} %bitcast.66) | data formatting | bytes 7340032 | tf_op jit(solution)/shard_map/reshape | solution.py:86
  167.6 6.6 %reshape.227 = bf16[1,4,14,1,64,512]{5,4,2,1,3,0:T(8,128)(2,1)} reshape(bf16[1,4,14,64,1,4,128]{6,5,3,2,1,4,0:T(4,128)(2,1)} %bitcast.65) | data formatting | bytes 7340032 | tf_op jit(solution)/shard_map/reshape | solution.py:91
  174.2 16.6 %all-gather.2.cloned.1.call-done = bf16[1,4,14,2,64,512]{5,4,2,1,0,3:T(8,128)(2,1)} async-done(((bf16[1,4,14,1,64,512]{5,4,2,1,0,3:T(8,128)(2,1)}), bf16[1,4,14,2,64,512]{5,4,2,1,0,3:T(8,128)(2,1)}) %all-gather.2.cloned.1.call-update) | async-done | bytes 7340048 | tf_op jit(solution)/shard_map/all_gather | solution.py:92
  190.8 7.1 %copy.70 = bf16[1,4,14,2,64,512]{5,4,3,2,1,0:T(8,128)(2,1)} copy(bf16[1,4,14,2,64,512]{5,4,2,1,0,3:T(8,128)(2,1)} %all-gather.2.cloned.1.call-done) | data formatting | bytes 14680064 | tf_op jit(solution)/shard_map/all_gather | solution.py:92
  (23 shorter events, 1.8 us)
Async XLA Ops:
  9.3 51.6 %all-to-all-start = ((s32[2,32,2]{1,0,2:T(2,128)}), s32[2,32,2]{1,0,2:T(2,128)S(1)}, u32[]{:S(2)}, u32[]{:S(2)}) async-start(s32[2,32,2]{1,0,2:T(2,128)} %broadcast_in_dim.62), calls=%async_computation | async-start | bytes 4096 | tf_op jit(solution)/shard_map/all_to_all | solution.py:59
  60.9 6.6 %all-to-all-start.3 = ((bf16[2,32,2,64,128]{4,3,1,0,2:T(8,128)(2,1)}), bf16[2,32,2,64,128]{4,3,1,0,2:T(8,128)(2,1)S(1)}, u32[]{:S(2)}, u32[]{:S(2)}) async-start(bf16[2,32,2,64,128]{4,3,1,0,2:T(8,128)(2,1)} %copy.65), calls=%async_computation.3 | async-start | bytes 4194304 | tf_op jit(solution)/shard_map/all_to_all | solution.py:58
  67.5 9.8 %all-to-all-start.1 = ((s32[4,1,1,32]{3,2,1,0:T(1,128)}), s32[4,1,1,32]{3,2,1,0:T(1,128)}, u32[]{:S(2)}, u32[]{:S(2)}) async-start(s32[4,1,1,32]{3,2,1,0:T(1,128)} %bitcast.4), calls=%async_computation.1 | async-start | bytes 4096 | tf_op jit(solution)/shard_map/all_to_all | solution.py:74
  77.4 10.4 %all-to-all-start.2 = ((s32[1,1,4,32]{3,1,0,2:T(1,128)}), s32[1,1,4,32]{3,1,0,2:T(1,128)S(1)}, u32[]{:S(2)}, u32[]{:S(2)}) async-start(s32[1,1,4,32]{3,1,0,2:T(1,128)} %bitcast.6), calls=%async_computation.2 | async-start | bytes 4096 | tf_op jit(solution)/shard_map/all_to_all | solution.py:73
  82.2 108.6 %all-gather.2.cloned.1.call-start = ((), (), s32[]{:S(2)}) async-start(), calls=%async_computation.6 | async-start | bytes 11010048 | tf_op jit(solution)/shard_map/all_gather | solution.py:92
Sparse Core Ops, SparseCore 0:
  174.3 16.4 all-gather.1
where the time goes:
time: 206 us; the launch traced here: 205 us
  blocking collectives  74.6 us (36%)
  local copies, waits for them, and re-layouts  62.8 us (30%)
  waiting for transfers between devices  23.1 us (11%)
  starting transfers between devices  17 us (8%)
  between operations  13.5 us (7%)
  other arithmetic  7.85 us (4%)
  matrix products  5.81 us (3%)
    all_to_all x1, blocking collectives, body(): lax.all_to_all(lax.all_to_all(chosen, 'expert', split_axis=0, concat_axis...  48.9 us
    all_to_all x1, blocking collectives, body(): lax.all_to_all(chosen, 'expert', split_axis=0, concat_axis=2, tiled=True)  25.7 us
    reshape x2, local copies, waits for them, and re-layouts, body(): trained.reshape(local_experts, block_rows, BLK, block_cols, BLK)  16.7 us
    all_gather x1, waiting for transfers between devices, body(): whole_rows = lax.all_gather(owned_rows, 'replica', axis=3, tiled=True)  16.6 us
    reshape x2, local copies, waits for them, and re-layouts, body(): snapshot.reshape(local_experts, block_rows, BLK, block_cols, BLK)  11.2 us
    all_gather x1, local copies, waits for them, and re-layouts, body(): whole_rows = lax.all_gather(owned_rows, 'replica', axis=3, tiled=True)  7.09 us
    reshape x1, local copies, waits for them, and re-layouts, body(): placed.reshape(owner_slots, source_count, block_rows, 1, part_rows, owner...  6.61 us
    gather x1, local copies, waits for them, and re-layouts, body(): trained.reshape(local_experts, block_rows, BLK, block_cols, BLK)  5.92 us
  transfers between devices with their start and end apart: 5, of which 4 were waited for; matrix products, arithmetic and copies ran while one was open for 27% of the time, Pallas kernels for 0%

commit v1 on v0

v1 whole, which is shorter than its diff:
```python
import functools
import math

import jax
import jax.numpy as jnp
from jax import lax
from jax.experimental import pallas as pl
from jax.experimental.pallas import tpu as pltpu
from jax.sharding import PartitionSpec as P

BLK = 128
TAG_ROWS = 16
SMEM = pl.BlockSpec(memory_space=pltpu.SMEM)
VMEM = pl.BlockSpec(memory_space=pltpu.VMEM)
HBM = pl.BlockSpec(memory_space=pltpu.MemorySpace.HBM)


def axis(name):
    return lax.axis_index(name).astype(jnp.int32)


def params(mib):
    return pltpu.CompilerParams(vmem_limit_bytes=mib << 20)


def cost(flops, moved):
    return pl.CostEstimate(flops=flops, bytes_accessed=moved, transcendentals=0)


def encode_kernel(rounds, halves, flags, new_hbm, old_hbm, *refs):
    outs, (spots, new, old, new_sem, old_sem) = refs[: 2 * len(rounds)], refs[2 * len(rounds) :]
    experts, block_cols, block_rows = flags.shape
    part = BLK // halves

    def scan(a, found):
        found = list(found)
        for c in range(block_cols):
            for p in range(experts):
                spots[p, found[p]] = a * block_cols + c
                found[p] = found[p] + flags[p, c, a]
        return tuple(found)

    totals = lax.fori_loop(0, block_rows, scan, (jnp.int32(0),) * experts, unroll=2)

    def bounds(p, lo, hi):
        return jnp.minimum(lo, totals[p]), jnp.minimum(hi, totals[p])

    def sides(p, j):
        lane = pl.ds(pl.multiple_of(j * BLK, BLK), BLK)
        return (
            (new_hbm, new.at[p, :, lane], new_sem.at[p, j]),
            (old_hbm, old.at[p, :, lane], old_sem.at[p, j]),
        )

    for lo, hi in rounds:
        for p in range(experts):

            @pl.loop(*bounds(p, lo, hi))
            def _(j, p=p):
                spot = spots[p, j]
                rows = pl.ds(pl.multiple_of((spot // block_cols) * BLK, BLK), BLK)
                cols = pl.ds(pl.multiple_of((spot % block_cols) * BLK, BLK), BLK)
                for source, target, sem in sides(p, j):
                    pltpu.make_async_copy(source.at[p, rows, cols], target, sem).start()

    row = lax.broadcasted_iota(jnp.int32, (BLK, 2 * BLK), 0)
    column = lax.broadcasted_iota(jnp.int32, (BLK, 2 * BLK), 1) % BLK
    common = row & column
    for shift in (4, 2, 1):
        common = common ^ (common >> shift)
    signs = (1 - 2 * (common & 1)).astype(jnp.float32).astype(jnp.bfloat16)
    first = axis("replica") == 0
    lanes = lax.broadcasted_iota(jnp.int32, (TAG_ROWS, BLK), 1)
    for p in range(experts):

        def tag(j, held, p=p):
            return jnp.where(lanes == j, spots[p, j], held)

        held = lax.fori_loop(0, totals[p], tag, jnp.where(lanes == BLK - 1, totals[p], -1))
        held = held.astype(jnp.float32).astype(jnp.bfloat16)
        for out in outs[:2]:
            out[p, pl.ds((rounds[0][1] - rounds[0][0]) * part, TAG_ROWS), :] = held

    for i, (lo, hi) in enumerate(rounds):
        own, oth = outs[2 * i : 2 * i + 2]
        for p in range(experts):

            @pl.loop(*bounds(p, lo, hi))
            def _(j, p=p):
                for source, target, sem in sides(p, j):
                    pltpu.make_async_copy(source.at[p, pl.ds(0, BLK), pl.ds(0, BLK)], target, sem).wait()

        for p in range(experts):
            delta = new[p, :, lo * BLK : hi * BLK] - old[p, :, lo * BLK : hi * BLK].astype(jnp.float32)
            high = delta.astype(jnp.bfloat16)
            low = (delta - high.astype(jnp.float32)).astype(jnp.bfloat16)
            coded = jnp.dot(signs, jnp.concatenate([high, low], axis=0), preferred_element_type=jnp.float32)
            coded = (coded * (1.0 / math.sqrt(BLK))).astype(jnp.bfloat16)
            for k in range(hi - lo):
                top = coded[:part, k * BLK : (k + 1) * BLK]
                bottom = coded[part:, k * BLK : (k + 1) * BLK]
                own[p, k * part : (k + 1) * part, :] = jnp.where(first, top, bottom)
                oth[p, k * part : (k + 1) * part, :] = jnp.where(first, bottom, top)


def encode(trained, snapshot, flags, rounds, halves):
    experts, block_cols, block_rows = flags.shape
    ranks = rounds[-1][1]
    outs = []
    for i, (lo, hi) in enumerate(rounds):
        rows = (hi - lo) * (BLK // halves) + (0 if i else TAG_ROWS)
        outs += [jax.ShapeDtypeStruct((experts, rows, BLK), jnp.bfloat16)] * 2
    space = pltpu.MemorySpace.HBM
    return pl.pallas_call(
        functools.partial(encode_kernel, rounds, halves),
        out_shape=outs,
        in_specs=[SMEM, HBM, HBM],
        out_specs=[VMEM] * len(outs),
        scratch_shapes=[
            pltpu.SMEM((experts, block_cols * block_rows + 1), jnp.int32),
            pltpu.VMEM((experts, BLK, ranks * BLK), jnp.float32),
            pltpu.VMEM((experts, BLK, ranks * BLK), jnp.bfloat16),
            pltpu.SemaphoreType.DMA((experts, ranks)),
            pltpu.SemaphoreType.DMA((experts, ranks)),
        ],
        compiler_params=params(24),
        cost_estimate=cost(4_000_000_000, 4_000_000),
        name="encode",
    )(
        flags,
        pltpu.with_memory_space_constraint(trained, space),
        pltpu.with_memory_space_constraint(snapshot, space),
    )


def by_slot_kernel(placement, own, got, *outs):
    experts = own.shape[0]
    core, expert = axis("replica"), axis("expert")
    for k, out in enumerate(outs):
        chosen = placement[expert ^ k]
        here, at = chosen // experts == core, chosen % experts

        @pl.when(here)
        def _(out=out, at=at):
            out[...] = own[at]

        @pl.when(jnp.logical_not(here))
        def _(out=out, at=at):
            out[...] = got[at]


def by_slot(placement, own, got, count):
    out = jax.ShapeDtypeStruct(own.shape[1:], own.dtype)
    return pl.pallas_call(
        by_slot_kernel,
        out_shape=(out,) * count,
        in_specs=[SMEM, VMEM, VMEM],
        out_specs=[VMEM] * count,
        compiler_params=params(16),
        cost_estimate=cost(1_000_000_000, 2_000_000),
        name="by_slot",
    )(placement, own, got)


def by_range_kernel(members, *refs):
    count = len(refs) * members // (members + 1)
    pieces, outs = refs[:count], refs[count:]
    rows = pieces[0].shape[0]
    shift = axis("expert") ^ (axis("tensor") * members)
    for case in range(count):

        @pl.when(shift == case)
        def _(case=case):
            for j, out in enumerate(outs):
                for u in range(members):
                    out[pl.ds(u * rows, rows), :] = pieces[case ^ (j * members + u)][...]


def by_range(pieces, members):
    rows, cols = pieces[0].shape
    out = jax.ShapeDtypeStruct((members * rows, cols), pieces[0].dtype)
    return pl.pallas_call(
        functools.partial(by_range_kernel, members),
        out_shape=(out,) * (len(pieces) // members),
        in_specs=[VMEM] * len(pieces),
        out_specs=[VMEM] * (len(pieces) // members),
        compiler_params=params(16),
        cost_estimate=cost(1_000_000_000, 2_000_000),
        name="by_range",
    )(*pieces)


def clear_kernel(out, zeros, sems):
    zeros[...] = jnp.zeros_like(zeros)
    step = zeros.shape[0]

    def blank(i):
        return pltpu.make_async_copy(zeros, out.at[0, pl.ds(i * step, step), :], sems.at[i])

    for i in range(out.shape[1] // step):
        blank(i).start()
    for i in range(out.shape[1] // step):
        blank(i).wait()


def clear(shape, step):
    return pl.pallas_call(
        clear_kernel,
        out_shape=jax.ShapeDtypeStruct(shape, jnp.bfloat16),
        out_specs=HBM,
        scratch_shapes=[pltpu.VMEM((step, shape[2]), jnp.bfloat16), pltpu.SemaphoreType.DMA((shape[1] // step,))],
        compiler_params=params(4),
        cost_estimate=cost(2_000_000_000, 7_000_000),
        name="clear",
    )()


def place_kernel(turns, members, lo, ranks, block_cols, local_rows, local_cols, tags, *refs):
    count = len(turns)
    mine, theirs = refs[:count], refs[count : 2 * count]
    out, sems = refs[-2:]
    part = BLK // 2
    rows_each = mine[0].shape[0] // members
    own_row = axis("replica") * part
    tensor = axis("tensor")
    spans = []
    for i, turn in enumerate(turns):
        for u in range(members):
            line = turn * members + u
            found = jnp.clip(tags[line, BLK - 1] - lo, 0, ranks)
            spans.append((i, u, found))

            @pl.loop(0, found)
            def _(j, i=i, u=u, turn=turn, line=line):
                spot = tags[line, lo + j]
                row = (tensor ^ turn) * local_rows + (spot // block_cols) * BLK
                cols = pl.ds(pl.multiple_of(u * local_cols + (spot % block_cols) * BLK, BLK), BLK)
                source = pl.ds(pl.multiple_of(u * rows_each + j * part, TAG_ROWS), part)
                for k, (held, start) in enumerate(((mine[i], own_row), (theirs[i], part - own_row))):
                    target = out.at[0, pl.ds(pl.multiple_of(row + start, part), part), cols]
                    pltpu.make_async_copy(held.at[source, :], target, sems.at[k, i * members + u, j]).start()

    for i, u, found in spans:

        @pl.loop(0, found)
        def _(j, i=i, u=u):
            for k, held in enumerate((mine[i], theirs[i])):
                target = out.at[0, pl.ds(0, part), pl.ds(0, BLK)]
                pltpu.make_async_copy(held.at[pl.ds(0, part), :], target, sems.at[k, i * members + u, j]).wait()


def place(out, tags, mine, theirs, turns, members, lo, ranks, block_cols, local_rows, local_cols):
    count = len(turns)
    return pl.pallas_call(
        functools.partial(place_kernel, turns, members, lo, ranks, block_cols, local_rows, local_cols),
        out_shape=jax.ShapeDtypeStruct(out.shape, out.dtype),
        in_specs=[SMEM] + [VMEM] * (2 * count) + [HBM],
        out_specs=HBM,
        scratch_shapes=[pltpu.SemaphoreType.DMA((2, count * members, ranks))],
        input_output_aliases={1 + 2 * count: 0},
        compiler_params=params(16),
        cost_estimate=cost(2_000_000_000, 4_000_000),
        name="place",
    )(tags, *mine, *theirs, out)


def push(trained, snapshot, changed, placement):
    _, local_rows, local_cols = trained.shape
    copies = lax.axis_size("replica")
    tensor_count = lax.axis_size("tensor")
    expert_count = lax.axis_size("expert")
    members = expert_count // tensor_count
    block_rows, block_cols = local_rows // BLK, local_cols // BLK
    block_count = block_rows * block_cols
    capacity = (4 * block_count + 3) // 7
    axes = ("expert", "tensor", "replica")

    def device(e, t, r):
        return (e * tensor_count + t) * copies + r

    def permute(array, target):
        pairs = [
            (device(e, t, r), device(*target(e, t, r)))
            for e in range(expert_count)
            for t in range(tensor_count)
            for r in range(copies)
        ]
        return lax.ppermute(array, axes, pairs)

    def swap(e, t, r):
        return e, t, 1 - r

    flags = jnp.transpose(changed, (0, 2, 1))
    first = max(1, capacity * 3 // 8)
    rounds = [(0, first), (first, capacity)]
    far = [j for j in range(tensor_count) if j > 1]
    coded = encode(trained, snapshot, flags, rounds, copies)
    swapped = [permute(coded[2 * i + 1], swap) for i in range(len(rounds))]
    out = clear((1, tensor_count * local_rows, members * local_cols), 256)
    tags = None
    for i, (lo, hi) in enumerate(rounds):
        pieces = list(by_slot(placement, coded[2 * i], swapped[i], expert_count))
        for k in range(1, expert_count):
            pieces[k] = permute(pieces[k], lambda e, t, r: (e ^ k, t, r))
        pieces = list(by_range(pieces, members))
        for j in far + [1]:
            pieces[j] = permute(pieces[j], lambda e, t, r: (e, t ^ j, r))
        theirs = [permute(piece, swap) for piece in pieces]
        if i == 0:
            rows_each = pieces[0].shape[0] // members
            lines = [piece[u * rows_each + (hi - lo) * (BLK // copies)] for piece in pieces for u in range(members)]
            tags = jnp.stack(lines).astype(jnp.int32)
        groups = [[0, 1] + far] if i == 0 else [[0, 1]] + [[j] for j in far[::-1]]
        for group in groups:
            out = place(
                out,
                tags,
                [pieces[j] for j in group],
                [theirs[j] for j in group],
                group,
                members,
                lo,
                hi - lo,
                block_cols,
                local_rows,
                local_cols,
            )
    return out


def solution(mesh):
    split = P("replica", "tensor", "expert")
    return jax.shard_map(
        push,
        mesh=mesh,
        in_specs=(split, split, split, P()),
        out_specs=P("expert", None, "tensor"),
        check_vma=False,
    )
```

time: 206 us -> 96.5 us (0.47)
  blocking collectives: 74.6 us -> 0 us
  local copies, waits for them, and re-layouts: 62.8 us -> 0.7 us
  waiting for transfers between devices: 23.1 us -> 58.2 us
  Pallas kernels: 0 us -> 17.9 us
  between operations: 13.5 us -> 0.16 us
  other arithmetic: 7.85 us -> 0.01 us
  matrix products: 5.81 us -> 0 us
  starting transfers between devices: 17 us -> 19.4 us
    all_to_all x2 -> x0, blocking collectives: 74.6 us -> none  [the longest x1 48.9 us: body(): lax.all_to_all(lax.all_to_all(chosen, 'expert', split_axis=0, concat_axis...]
    ppermute x0 -> x22, waiting for transfers between devices: none -> 58.2 us  [permute(): return lax.ppermute(array, axes, pairs)]
    reshape x9 -> x0, local copies, waits for them, and re-layouts: 40.1 us -> none  [the longest x2 16.7 us: body(): trained.reshape(local_experts, block_rows, BLK, block_cols, BLK)]
    ppermute x0 -> x22, starting transfers between devices: none -> 19.4 us  [permute(): return lax.ppermute(array, axes, pairs)]
    pallas_call x0 -> x10, Pallas kernels: none -> 17.9 us  [the longest x4 7.91 us: place(): pl.pallas_call(functools.partial(place_kernel, turns, members, lo, ranks,...]
    all_to_all x4 -> x0, starting transfers between devices: 17 us -> none  [the longest x1 5.19 us: body(): lax.all_to_all(chosen_spots, 'expert', split_axis=0, concat_axis=2, tiled...]
    all_gather x1 -> x0, waiting for transfers between devices: 16.6 us -> none  [body(): whole_rows = lax.all_gather(owned_rows, 'replica', axis=3, tiled=True)]
    gather x7 -> x0, local copies, waits for them, and re-layouts: 12.7 us -> none  [the longest x1 5.92 us: body(): trained.reshape(local_experts, block_rows, BLK, block_cols, BLK)]
  transfers between devices with their start and end apart: 5 -> 22, of which waited for: 4 -> 8; matrix products, arithmetic and copies ran while one was open for 27% -> 0% of each run, Pallas kernels for 0% -> 12%
where the time goes in v1:
time: 96.5 us; the launch traced here: 96.3 us
  waiting for transfers between devices  58.2 us (60%)
  starting transfers between devices  19.4 us (20%)
  Pallas kernels  17.9 us (19%)
    ppermute x22, waiting for transfers between devices, permute(): return lax.ppermute(array, axes, pairs)  58.2 us
    ppermute x22, starting transfers between devices, permute(): return lax.ppermute(array, axes, pairs)  19.4 us
    pallas_call x4, Pallas kernels, place(): pl.pallas_call(functools.partial(place_kernel, turns, members, lo, ranks,...  7.91 us
    pallas_call x1, Pallas kernels, encode(): pl.pallas_call(functools.partial(encode_kernel, rounds, halves), out_shap...  5.26 us
    pallas_call x1, Pallas kernels, clear(): pl.pallas_call(clear_kernel, out_shape=jax.ShapeDtypeStruct(shape, jnp.bf...  3.2 us
  transfers between devices with their start and end apart: 22, of which 8 were waited for; matrix products, arithmetic and copies ran while one was open for 0% of the time, Pallas kernels for 12%

profile of v1, /device:TPU:0, one launch (start us, length us, event | category | flops | bytes accessed | tf_op | source)
XLA Modules:
  0.0 96.3 jit_solution(3001104199157310970)
XLA Ops:
  0.0 0.7 copy-done
  0.7 5.3 %encode.1 = (bf16[2,784,128]{2,1,0:T(8,128)(2,1)S(1)}, bf16[2,784,128]{2,1,0:T(8,128)(2,1)S(1)}, bf16[2,1280,128]{2,1,0:T(8,128)(2,1)S(1)}, bf16[2,1280,128]{2,1,0:T(8,128)(2,1)S(1)}) custom-call(s32[2,4,14]{2,1,0:T(4,128)S(1)} %bitcast.1, f32[2,1792,512]{2,1,0:T(8,128)} %new_hbm.1, bf16[2,1792,512]{2,1,0:T(8,128)(2,1)} %old_hbm.1), custom_call_target="tpu_custom_call" | custom-call | flops 4000000000 | bytes 4000000 | tf_op jit(solution)/shard_map/encode/pallas_call | solution.py:114
  6.0 0.3 collective-permute-start.7
  6.3 0.3 collective-permute-start
  6.5 2.2 %collective-permute-done.got = bf16[2,784,128]{2,1,0:T(8,128)(2,1)S(1)} collective-permute-done((bf16[2,784,128]{2,1,0:T(8,128)(2,1)S(1)}, bf16[2,784,128]{2,1,0:T(8,128)(2,1)S(1)}, u32[]{:S(2)}, u32[]{:S(2)}) %collective-permute-start) | collective-permute-done | bytes 401440 | tf_op jit(solution)/shard_map/ppermute | solution.py:288
  8.7 0.7 by_slot.2
  9.4 2.6 %collective-permute-start.1 = (bf16[784,128]{1,0:T(8,128)(2,1)S(1)}, bf16[784,128]{1,0:T(8,128)(2,1)S(1)}, u32[]{:S(2)}, u32[]{:S(2)}) collective-permute-start(bf16[784,128]{1,0:T(8,128)(2,1)S(1)} %get-tuple-element.28), channel_id=1, source_target_pairs={{0,8},{1,9},{2,10},{3,11},{4,12},{5,13},{6,14},{7,15},{8,0},{9,1},... | collective-permute-start | bytes 602120 | tf_op jit(solution)/shard_map/ppermute | solution.py:288
  12.0 0.7 by_slot.3
  12.7 2.2 %collective-permute-start.10 = (bf16[1280,128]{1,0:T(8,128)(2,1)S(1)}, bf16[1280,128]{1,0:T(8,128)(2,1)S(1)}, u32[]{:S(2)}, u32[]{:S(2)}) collective-permute-start(bf16[1280,128]{1,0:T(8,128)(2,1)S(1)} %get-tuple-element.40), channel_id=1, source_target_pairs={{0,24},{1,25},{2,26},{3,27},{4,28},{5,29},{6,30},{7,31},{8,16},{9,... | collective-permute-start | bytes 983048 | tf_op jit(solution)/shard_map/ppermute | solution.py:288
  14.9 0.6 collective-permute-start.8
  15.5 0.7 collective-permute-start.9
  16.3 1.3 %collective-permute-start.2 = (bf16[784,128]{1,0:T(8,128)(2,1)S(1)}, bf16[784,128]{1,0:T(8,128)(2,1)S(1)}, u32[]{:S(2)}, u32[]{:S(2)}) collective-permute-start(bf16[784,128]{1,0:T(8,128)(2,1)S(1)} %get-tuple-element.29), channel_id=1, source_target_pairs={{0,16},{1,17},{2,18},{3,19},{4,20},{5,21},{6,22},{7,23},{8,24},{9,... | collective-permute-start | bytes 602120 | tf_op jit(solution)/shard_map/ppermute | solution.py:288
  17.6 0.3 collective-permute-done.1.refs_1_
  17.8 2.8 %collective-permute-start.3 = (bf16[784,128]{1,0:T(8,128)(2,1)S(1)}, bf16[784,128]{1,0:T(8,128)(2,1)S(1)}, u32[]{:S(2)}, u32[]{:S(2)}) collective-permute-start(bf16[784,128]{1,0:T(8,128)(2,1)S(1)} %get-tuple-element.30), channel_id=1, source_target_pairs={{0,24},{1,25},{2,26},{3,27},{4,28},{5,29},{6,30},{7,31},{8,16},{9,... | collective-permute-start | bytes 602120 | tf_op jit(solution)/shard_map/ppermute | solution.py:288
  20.6 19.5 %collective-permute-done.2.refs_2_ = bf16[784,128]{1,0:T(8,128)(2,1)S(1)} collective-permute-done((bf16[784,128]{1,0:T(8,128)(2,1)S(1)}, bf16[784,128]{1,0:T(8,128)(2,1)S(1)}, u32[]{:S(2)}, u32[]{:S(2)}) %collective-permute-start.2) | collective-permute-done | bytes 200736 | tf_op jit(solution)/shard_map/ppermute | solution.py:288
  40.1 2.3 %collective-permute-start.4 = (bf16[784,128]{1,0:T(8,128)(2,1)S(1)}, bf16[784,128]{1,0:T(8,128)(2,1)S(1)}, u32[]{:S(2)}, u32[]{:S(2)}) collective-permute-start(bf16[784,128]{1,0:T(8,128)(2,1)S(1)} %get-tuple-element.32), channel_id=1, source_target_pairs={{0,2},{1,3},{2,0},{3,1},{4,6},{5,7},{6,4},{7,5},{8,10},{9,11},{10,... | collective-permute-start | bytes 602120 | tf_op jit(solution)/shard_map/ppermute | solution.py:288
  42.4 2.8 %collective-permute-start.5 = (bf16[784,128]{1,0:T(8,128)(2,1)S(1)}, bf16[784,128]{1,0:T(8,128)(2,1)S(1)}, u32[]{:S(2)}, u32[]{:S(2)}) collective-permute-start(bf16[784,128]{1,0:T(8,128)(2,1)S(1)} %get-tuple-element.33), channel_id=1, source_target_pairs={{0,4},{1,5},{2,6},{3,7},{4,0},{5,1},{6,2},{7,3},{8,12},{9,13},{10,... | collective-permute-start | bytes 602120 | tf_op jit(solution)/shard_map/ppermute | solution.py:288
  45.3 0.4 collective-permute-start.15
  45.7 1.3 %collective-permute-start.6 = (bf16[784,128]{1,0:T(8,128)(2,1)S(1)}, bf16[784,128]{1,0:T(8,128)(2,1)S(1)}, u32[]{:S(2)}, u32[]{:S(2)}) collective-permute-start(bf16[784,128]{1,0:T(8,128)(2,1)S(1)} %get-tuple-element.34), channel_id=1, source_target_pairs={{0,6},{1,7},{2,4},{3,5},{4,2},{5,3},{6,0},{7,1},{8,14},{9,15},{10,... | collective-permute-start | bytes 602120 | tf_op jit(solution)/shard_map/ppermute | solution.py:288
  47.0 4.6 %collective-permute-done.4.refs_1_ = bf16[784,128]{1,0:T(8,128)(2,1)S(1)} collective-permute-done((bf16[784,128]{1,0:T(8,128)(2,1)S(1)}, bf16[784,128]{1,0:T(8,128)(2,1)S(1)}, u32[]{:S(2)}, u32[]{:S(2)}) %collective-permute-start.4) | collective-permute-done | bytes 200736 | tf_op jit(solution)/shard_map/ppermute | solution.py:288
  51.6 3.9 %collective-permute-done.5.refs_2_ = bf16[784,128]{1,0:T(8,128)(2,1)S(1)} collective-permute-done((bf16[784,128]{1,0:T(8,128)(2,1)S(1)}, bf16[784,128]{1,0:T(8,128)(2,1)S(1)}, u32[]{:S(2)}, u32[]{:S(2)}) %collective-permute-start.5) | collective-permute-done | bytes 200736 | tf_op jit(solution)/shard_map/ppermute | solution.py:288
  55.4 9.4 %collective-permute-done.6.refs_3_ = bf16[784,128]{1,0:T(8,128)(2,1)S(1)} collective-permute-done((bf16[784,128]{1,0:T(8,128)(2,1)S(1)}, bf16[784,128]{1,0:T(8,128)(2,1)S(1)}, u32[]{:S(2)}, u32[]{:S(2)}) %collective-permute-start.6) | collective-permute-done | bytes 200736 | tf_op jit(solution)/shard_map/ppermute | solution.py:288
  64.8 1.2 %collective-permute-start.13 = (bf16[1280,128]{1,0:T(8,128)(2,1)S(1)}, bf16[1280,128]{1,0:T(8,128)(2,1)S(1)}, u32[]{:S(2)}, u32[]{:S(2)}) collective-permute-start(bf16[1280,128]{1,0:T(8,128)(2,1)S(1)} %get-tuple-element.42), channel_id=1, source_target_pairs={{0,6},{1,7},{2,4},{3,5},{4,2},{5,3},{6,0},{7,1},{8,14},{9,15},{10,... | collective-permute-start | bytes 983048 | tf_op jit(solution)/shard_map/ppermute | solution.py:288
  66.0 0.5 collective-permute-start.16
  66.5 0.2 collective-permute-start.17
  66.7 3.2 %clear.1.refs_8_ = bf16[1,7168,512]{2,1,0:T(8,128)(2,1)} custom-call(), custom_call_target="tpu_custom_call" | custom-call | flops 2000000000 | bytes 7000000 | tf_op jit(solution)/shard_map/clear/pallas_call | solution.py:207
  70.0 7.3 %collective-permute-done.13.refs_0_ = bf16[1280,128]{1,0:T(8,128)(2,1)S(1)} collective-permute-done((bf16[1280,128]{1,0:T(8,128)(2,1)S(1)}, bf16[1280,128]{1,0:T(8,128)(2,1)S(1)}, u32[]{:S(2)}, u32[]{:S(2)}) %collective-permute-start.13) | collective-permute-done | bytes 327712 | tf_op jit(solution)/shard_map/ppermute | solution.py:288
  77.3 2.9 %place.4.refs_4_ = bf16[1,7168,512]{2,1,0:T(8,128)(2,1)} custom-call(s32[4,128]{1,0:T(4,128)S(1)} %maximum_convert_fusion.tags, bf16[784,128]{1,0:T(8,128)(2,1)S(1)} %get-tuple-element.31.refs_0_, bf16[784,128]{1,0:T(8,128)(2,1)S(1)} %collective-permute-done.4.refs_1_, ...), custom_call_target="tpu_custom_call", output_to_operand_aliasing={{}: (9, {})} | custom-call | flops 2000000000 | bytes 4000000 | tf_op jit(solution)/shard_map/place/pallas_call | solution.py:254
  80.1 11.1 %collective-permute-done.11.refs_0_ = bf16[1280,128]{1,0:T(8,128)(2,1)S(1)} collective-permute-done((bf16[1280,128]{1,0:T(8,128)(2,1)S(1)}, bf16[1280,128]{1,0:T(8,128)(2,1)S(1)}, u32[]{:S(2)}, u32[]{:S(2)}) %collective-permute-start.11) | collective-permute-done | bytes 327712 | tf_op jit(solution)/shard_map/ppermute | solution.py:288
  91.3 2.5 %place.5.refs_2_ = bf16[1,7168,512]{2,1,0:T(8,128)(2,1)} custom-call(s32[4,128]{1,0:T(4,128)S(1)} %maximum_convert_fusion.tags, bf16[1280,128]{1,0:T(8,128)(2,1)S(1)} %get-tuple-element.43.refs_0_, bf16[1280,128]{1,0:T(8,128)(2,1)S(1)} %collective-permute-done.15.refs_1_, ...), custom_call_target="tpu_custom_call", output_to_operand_aliasing={{}: (5, {})} | custom-call | flops 2000000000 | bytes 4000000 | tf_op jit(solution)/shard_map/place/pallas_call | solution.py:254
  93.8 1.6 %place.6.refs_2_ = bf16[1,7168,512]{2,1,0:T(8,128)(2,1)} custom-call(s32[4,128]{1,0:T(4,128)S(1)} %maximum_convert_fusion.tags, bf16[1280,128]{1,0:T(8,128)(2,1)S(1)} %collective-permute-done.13.refs_0_, bf16[1280,128]{1,0:T(8,128)(2,1)S(1)} %collective-permute-done.14.refs_1_, bf16[1,7168,512]{2,1,0:T(8,128)(2,1)} %place.5.refs_2_), custom_call_target="tpu_custom_call", output_to_operand_aliasing={{}: (3, {})} | custom-call | flops 2000000000 | bytes 4000000 | tf_op jit(solution)/shard_map/place/pallas_call | solution.py:254
  95.4 0.9 place.7
  (31 shorter events, 0.3 us)
Async XLA Ops:
  0.0 0.7 copy-start
  0.7 8.0 %copy-start.1 = (s32[4]{0:T(128)S(1)}, s32[4]{0:T(128)}, u32[]{:S(2)}) copy-start(s32[4]{0:T(128)} %placement.3) | copy-start | bytes 52
  6.0 6.0 %collective-permute-start.7 = (bf16[2,1280,128]{2,1,0:T(8,128)(2,1)S(1)}, bf16[2,1280,128]{2,1,0:T(8,128)(2,1)S(1)}, u32[]{:S(2)}, u32[]{:S(2)}) collective-permute-start(bf16[2,1280,128]{2,1,0:T(8,128)(2,1)S(1)} %get-tuple-element.36), channel_id=1, source_target_pairs={{0,1},{1,0},{2,3},{3,2},{4,5},{5,4},{6,7},{7,6},{8,9},{9,8},{10,11... | collective-permute-start | bytes 1966088 | tf_op jit(solution)/shard_map/ppermute | solution.py:288
  6.3 2.4 %collective-permute-start = (bf16[2,784,128]{2,1,0:T(8,128)(2,1)S(1)}, bf16[2,784,128]{2,1,0:T(8,128)(2,1)S(1)}, u32[]{:S(2)}, u32[]{:S(2)}) collective-permute-start(bf16[2,784,128]{2,1,0:T(8,128)(2,1)S(1)} %get-tuple-element.26), channel_id=1, source_target_pairs={{0,1},{1,0},{2,3},{3,2},{4,5},{5,4},{6,7},{7,6},{8,9},{9,8},{10,11... | collective-permute-start | bytes 1204232 | tf_op jit(solution)/shard_map/ppermute | solution.py:288
  9.4 8.4 %collective-permute-start.1 = (bf16[784,128]{1,0:T(8,128)(2,1)S(1)}, bf16[784,128]{1,0:T(8,128)(2,1)S(1)}, u32[]{:S(2)}, u32[]{:S(2)}) collective-permute-start(bf16[784,128]{1,0:T(8,128)(2,1)S(1)} %get-tuple-element.28), channel_id=1, source_target_pairs={{0,8},{1,9},{2,10},{3,11},{4,12},{5,13},{6,14},{7,15},{8,0},{9,1},... | collective-permute-start | bytes 602120 | tf_op jit(solution)/shard_map/ppermute | solution.py:288
  12.7 32.5 %collective-permute-start.10 = (bf16[1280,128]{1,0:T(8,128)(2,1)S(1)}, bf16[1280,128]{1,0:T(8,128)(2,1)S(1)}, u32[]{:S(2)}, u32[]{:S(2)}) collective-permute-start(bf16[1280,128]{1,0:T(8,128)(2,1)S(1)} %get-tuple-element.40), channel_id=1, source_target_pairs={{0,24},{1,25},{2,26},{3,27},{4,28},{5,29},{6,30},{7,31},{8,16},{9,... | collective-permute-start | bytes 983048 | tf_op jit(solution)/shard_map/ppermute | solution.py:288
  14.9 30.3 %collective-permute-start.8 = (bf16[1280,128]{1,0:T(8,128)(2,1)S(1)}, bf16[1280,128]{1,0:T(8,128)(2,1)S(1)}, u32[]{:S(2)}, u32[]{:S(2)}) collective-permute-start(bf16[1280,128]{1,0:T(8,128)(2,1)S(1)} %get-tuple-element.38), channel_id=1, source_target_pairs={{0,8},{1,9},{2,10},{3,11},{4,12},{5,13},{6,14},{7,15},{8,0},{9,1},... | collective-permute-start | bytes 983048 | tf_op jit(solution)/shard_map/ppermute | solution.py:288
  15.5 29.6 %collective-permute-start.9 = (bf16[1280,128]{1,0:T(8,128)(2,1)S(1)}, bf16[1280,128]{1,0:T(8,128)(2,1)S(1)}, u32[]{:S(2)}, u32[]{:S(2)}) collective-permute-start(bf16[1280,128]{1,0:T(8,128)(2,1)S(1)} %get-tuple-element.39), channel_id=1, source_target_pairs={{0,16},{1,17},{2,18},{3,19},{4,20},{5,21},{6,22},{7,23},{8,24},{9,... | collective-permute-start | bytes 983048 | tf_op jit(solution)/shard_map/ppermute | solution.py:288
  16.3 23.8 %collective-permute-start.2 = (bf16[784,128]{1,0:T(8,128)(2,1)S(1)}, bf16[784,128]{1,0:T(8,128)(2,1)S(1)}, u32[]{:S(2)}, u32[]{:S(2)}) collective-permute-start(bf16[784,128]{1,0:T(8,128)(2,1)S(1)} %get-tuple-element.29), channel_id=1, source_target_pairs={{0,16},{1,17},{2,18},{3,19},{4,20},{5,21},{6,22},{7,23},{8,24},{9,... | collective-permute-start | bytes 602120 | tf_op jit(solution)/shard_map/ppermute | solution.py:288
  17.8 22.3 %collective-permute-start.3 = (bf16[784,128]{1,0:T(8,128)(2,1)S(1)}, bf16[784,128]{1,0:T(8,128)(2,1)S(1)}, u32[]{:S(2)}, u32[]{:S(2)}) collective-permute-start(bf16[784,128]{1,0:T(8,128)(2,1)S(1)} %get-tuple-element.30), channel_id=1, source_target_pairs={{0,24},{1,25},{2,26},{3,27},{4,28},{5,29},{6,30},{7,31},{8,16},{9,... | collective-permute-start | bytes 602120 | tf_op jit(solution)/shard_map/ppermute | solution.py:288
  40.1 11.4 %collective-permute-start.4 = (bf16[784,128]{1,0:T(8,128)(2,1)S(1)}, bf16[784,128]{1,0:T(8,128)(2,1)S(1)}, u32[]{:S(2)}, u32[]{:S(2)}) collective-permute-start(bf16[784,128]{1,0:T(8,128)(2,1)S(1)} %get-tuple-element.32), channel_id=1, source_target_pairs={{0,2},{1,3},{2,0},{3,1},{4,6},{5,7},{6,4},{7,5},{8,10},{9,11},{10,... | collective-permute-start | bytes 602120 | tf_op jit(solution)/shard_map/ppermute | solution.py:288
  42.4 13.0 %collective-permute-start.5 = (bf16[784,128]{1,0:T(8,128)(2,1)S(1)}, bf16[784,128]{1,0:T(8,128)(2,1)S(1)}, u32[]{:S(2)}, u32[]{:S(2)}) collective-permute-start(bf16[784,128]{1,0:T(8,128)(2,1)S(1)} %get-tuple-element.33), channel_id=1, source_target_pairs={{0,4},{1,5},{2,6},{3,7},{4,0},{5,1},{6,2},{7,3},{8,12},{9,13},{10,... | collective-permute-start | bytes 602120 | tf_op jit(solution)/shard_map/ppermute | solution.py:288
  45.3 21.2 %collective-permute-start.15 = (bf16[1280,128]{1,0:T(8,128)(2,1)S(1)}, bf16[1280,128]{1,0:T(8,128)(2,1)S(1)}, u32[]{:S(2)}, u32[]{:S(2)}) collective-permute-start(bf16[1280,128]{1,0:T(8,128)(2,1)S(1)} %get-tuple-element.44), channel_id=1, source_target_pairs={{0,2},{1,3},{2,0},{3,1},{4,6},{5,7},{6,4},{7,5},{8,10},{9,11},{10,... | collective-permute-start | bytes 983048 | tf_op jit(solution)/shard_map/ppermute | solution.py:288
  45.7 19.1 %collective-permute-start.6 = (bf16[784,128]{1,0:T(8,128)(2,1)S(1)}, bf16[784,128]{1,0:T(8,128)(2,1)S(1)}, u32[]{:S(2)}, u32[]{:S(2)}) collective-permute-start(bf16[784,128]{1,0:T(8,128)(2,1)S(1)} %get-tuple-element.34), channel_id=1, source_target_pairs={{0,6},{1,7},{2,4},{3,5},{4,2},{5,3},{6,0},{7,1},{8,14},{9,15},{10,... | collective-permute-start | bytes 602120 | tf_op jit(solution)/shard_map/ppermute | solution.py:288
  47.0 19.0 %collective-permute-start.18 = (bf16[784,128]{1,0:T(8,128)(2,1)S(1)}, bf16[784,128]{1,0:T(8,128)(2,1)S(1)}, u32[]{:S(2)}, u32[]{:S(2)}) collective-permute-start(bf16[784,128]{1,0:T(8,128)(2,1)S(1)} %get-tuple-element.31.refs_0_), channel_id=1, source_target_pairs={{0,1},{1,0},{2,3},{3,2},{4,5},{5,4},{6,7},{7,6},{8,9},{9,8},{10,11... | collective-permute-start | bytes 602120 | tf_op jit(solution)/shard_map/ppermute | solution.py:288
  51.6 14.4 %collective-permute-start.19 = (bf16[784,128]{1,0:T(8,128)(2,1)S(1)}, bf16[784,128]{1,0:T(8,128)(2,1)S(1)}, u32[]{:S(2)}, u32[]{:S(2)}) collective-permute-start(bf16[784,128]{1,0:T(8,128)(2,1)S(1)} %collective-permute-done.4.refs_1_), channel_id=1, source_target_pairs={{0,1},{1,0},{2,3},{3,2},{4,5},{5,4},{6,7},{7,6},{8,9},{9,8},{10,11... | collective-permute-start | bytes 602120 | tf_op jit(solution)/shard_map/ppermute | solution.py:288
  55.4 11.1 %collective-permute-start.20 = (bf16[784,128]{1,0:T(8,128)(2,1)S(1)}, bf16[784,128]{1,0:T(8,128)(2,1)S(1)}, u32[]{:S(2)}, u32[]{:S(2)}) collective-permute-start(bf16[784,128]{1,0:T(8,128)(2,1)S(1)} %collective-permute-done.5.refs_2_), channel_id=1, source_target_pairs={{0,1},{1,0},{2,3},{3,2},{4,5},{5,4},{6,7},{7,6},{8,9},{9,8},{10,11... | collective-permute-start | bytes 602120 | tf_op jit(solution)/shard_map/ppermute | solution.py:288
  64.8 12.4 %collective-permute-start.13 = (bf16[1280,128]{1,0:T(8,128)(2,1)S(1)}, bf16[1280,128]{1,0:T(8,128)(2,1)S(1)}, u32[]{:S(2)}, u32[]{:S(2)}) collective-permute-start(bf16[1280,128]{1,0:T(8,128)(2,1)S(1)} %get-tuple-element.42), channel_id=1, source_target_pairs={{0,6},{1,7},{2,4},{3,5},{4,2},{5,3},{6,0},{7,1},{8,14},{9,15},{10,... | collective-permute-start | bytes 983048 | tf_op jit(solution)/shard_map/ppermute | solution.py:288
  66.0 11.2 %collective-permute-start.21 = (bf16[784,128]{1,0:T(8,128)(2,1)S(1)}, bf16[784,128]{1,0:T(8,128)(2,1)S(1)}, u32[]{:S(2)}, u32[]{:S(2)}) collective-permute-start(bf16[784,128]{1,0:T(8,128)(2,1)S(1)} %collective-permute-done.6.refs_3_), channel_id=1, source_target_pairs={{0,1},{1,0},{2,3},{3,2},{4,5},{5,4},{6,7},{7,6},{8,9},{9,8},{10,11... | collective-permute-start | bytes 602120 | tf_op jit(solution)/shard_map/ppermute | solution.py:288
  66.0 25.2 %collective-permute-start.16 = (bf16[1280,128]{1,0:T(8,128)(2,1)S(1)}, bf16[1280,128]{1,0:T(8,128)(2,1)S(1)}, u32[]{:S(2)}, u32[]{:S(2)}) collective-permute-start(bf16[1280,128]{1,0:T(8,128)(2,1)S(1)} %get-tuple-element.43.refs_0_), channel_id=1, source_target_pairs={{0,1},{1,0},{2,3},{3,2},{4,5},{5,4},{6,7},{7,6},{8,9},{9,8},{10,11... | collective-permute-start | bytes 983048 | tf_op jit(solution)/shard_map/ppermute | solution.py:288
  66.5 24.7 %collective-permute-start.11 = (bf16[1280,128]{1,0:T(8,128)(2,1)S(1)}, bf16[1280,128]{1,0:T(8,128)(2,1)S(1)}, u32[]{:S(2)}, u32[]{:S(2)}) collective-permute-start(bf16[1280,128]{1,0:T(8,128)(2,1)S(1)} %get-tuple-element.41), channel_id=1, source_target_pairs={{0,4},{1,5},{2,6},{3,7},{4,0},{5,1},{6,2},{7,3},{8,12},{9,13},{10,... | collective-permute-start | bytes 983048 | tf_op jit(solution)/shard_map/ppermute | solution.py:288
  66.5 24.7 %collective-permute-start.17 = (bf16[1280,128]{1,0:T(8,128)(2,1)S(1)}, bf16[1280,128]{1,0:T(8,128)(2,1)S(1)}, u32[]{:S(2)}, u32[]{:S(2)}) collective-permute-start(bf16[1280,128]{1,0:T(8,128)(2,1)S(1)} %collective-permute-done.15.refs_1_), channel_id=1, source_target_pairs={{0,1},{1,0},{2,3},{3,2},{4,5},{5,4},{6,7},{7,6},{8,9},{9,8},{10,11... | collective-permute-start | bytes 983048 | tf_op jit(solution)/shard_map/ppermute | solution.py:288
  77.2 16.5 %collective-permute-start.14 = (bf16[1280,128]{1,0:T(8,128)(2,1)S(1)}, bf16[1280,128]{1,0:T(8,128)(2,1)S(1)}, u32[]{:S(2)}, u32[]{:S(2)}) collective-permute-start(bf16[1280,128]{1,0:T(8,128)(2,1)S(1)} %collective-permute-done.13.refs_0_), channel_id=1, source_target_pairs={{0,1},{1,0},{2,3},{3,2},{4,5},{5,4},{6,7},{7,6},{8,9},{9,8},{10,11... | collective-permute-start | bytes 983048 | tf_op jit(solution)/shard_map/ppermute | solution.py:288
  91.2 4.1 %collective-permute-start.12 = (bf16[1280,128]{1,0:T(8,128)(2,1)S(1)}, bf16[1280,128]{1,0:T(8,128)(2,1)S(1)}, u32[]{:S(2)}, u32[]{:S(2)}) collective-permute-start(bf16[1280,128]{1,0:T(8,128)(2,1)S(1)} %collective-permute-done.11.refs_0_), channel_id=1, source_target_pairs={{0,1},{1,0},{2,3},{3,2},{4,5},{5,4},{6,7},{7,6},{8,9},{9,8},{10,11... | collective-permute-start | bytes 983048 | tf_op jit(solution)/shard_map/ppermute | solution.py:288

commit v2 on v1

v2 whole, which is shorter than its diff:
```python
import functools
import math

import jax
import jax.numpy as jnp
from jax import lax
from jax.experimental import pallas as pl
from jax.experimental.pallas import tpu as pltpu
from jax.sharding import PartitionSpec as P

BLK = 128
TAG_ROWS = 16
SMEM = pl.BlockSpec(memory_space=pltpu.SMEM)
VMEM = pl.BlockSpec(memory_space=pltpu.VMEM)
HBM = pl.BlockSpec(memory_space=pltpu.MemorySpace.HBM)


def axis(name):
    return lax.axis_index(name).astype(jnp.int32)


def params(mib):
    return pltpu.CompilerParams(vmem_limit_bytes=mib << 20)


def cost(flops, moved):
    return pl.CostEstimate(flops=flops, bytes_accessed=moved, transcendentals=0)


def encode_kernel(lo, hi, tagged, halves, flags_hbm, new_hbm, old_hbm, own, oth, flags, spots, new, old, flag_sem, new_sem, old_sem):
    copy = pltpu.make_async_copy(flags_hbm, flags, flag_sem)
    copy.start()
    experts, block_cols, block_rows = flags.shape
    part = BLK // halves
    row = lax.broadcasted_iota(jnp.int32, (BLK, 2 * BLK), 0)
    column = lax.broadcasted_iota(jnp.int32, (BLK, 2 * BLK), 1) % BLK
    common = row & column
    for shift in (4, 2, 1):
        common = common ^ (common >> shift)
    signs = (1 - 2 * (common & 1)).astype(jnp.float32).astype(jnp.bfloat16)
    first = axis("replica") == 0
    lanes = lax.broadcasted_iota(jnp.int32, (TAG_ROWS, BLK), 1)
    copy.wait()

    def scan(a, found):
        found = list(found)
        for c in range(block_cols):
            for p in range(experts):
                spots[p, found[p]] = a * block_cols + c
                found[p] = found[p] + flags[p, c, a]
        return tuple(found)

    totals = lax.fori_loop(0, block_rows, scan, (jnp.int32(0),) * experts, unroll=2)
    counts = [jnp.clip(total - lo, 0, hi - lo) for total in totals]

    def sides(p, j):
        lane = pl.ds(pl.multiple_of(j * BLK, BLK), BLK)
        return (
            (new_hbm, new.at[p, :, lane], new_sem.at[p, j]),
            (old_hbm, old.at[p, :, lane], old_sem.at[p, j]),
        )

    for p in range(experts):

        @pl.loop(0, counts[p])
        def _(j, p=p):
            spot = spots[p, lo + j]
            rows = pl.ds(pl.multiple_of((spot // block_cols) * BLK, BLK), BLK)
            cols = pl.ds(pl.multiple_of((spot % block_cols) * BLK, BLK), BLK)
            for source, target, sem in sides(p, j):
                pltpu.make_async_copy(source.at[p, rows, cols], target, sem).start()

    for p in range(experts if tagged else 0):

        def tag(j, held, p=p):
            return jnp.where(lanes == j, spots[p, j], held)

        held = lax.fori_loop(0, totals[p], tag, jnp.where(lanes == BLK - 1, totals[p], -1))
        held = held.astype(jnp.float32).astype(jnp.bfloat16)
        for out in (own, oth):
            out[p, pl.ds((hi - lo) * part, TAG_ROWS), :] = held

    for p in range(experts):

        @pl.loop(0, counts[p])
        def _(j, p=p):
            for source, target, sem in sides(p, j):
                pltpu.make_async_copy(source.at[p, pl.ds(0, BLK), pl.ds(0, BLK)], target, sem).wait()

        delta = new[p] - old[p].astype(jnp.float32)
        high = delta.astype(jnp.bfloat16)
        low = (delta - high.astype(jnp.float32)).astype(jnp.bfloat16)
        coded = jnp.dot(signs, jnp.concatenate([high, low], axis=0), preferred_element_type=jnp.float32)
        coded = (coded * (1.0 / math.sqrt(BLK))).astype(jnp.bfloat16)
        for k in range(hi - lo):
            top = coded[:part, k * BLK : (k + 1) * BLK]
            bottom = coded[part:, k * BLK : (k + 1) * BLK]
            own[p, k * part : (k + 1) * part, :] = jnp.where(first, top, bottom)
            oth[p, k * part : (k + 1) * part, :] = jnp.where(first, bottom, top)


def encode(trained, snapshot, flags, lo, hi, tagged, halves):
    experts, block_cols, block_rows = flags.shape
    ranks = hi - lo
    rows = ranks * (BLK // halves) + (TAG_ROWS if tagged else 0)
    out = jax.ShapeDtypeStruct((experts, rows, BLK), jnp.bfloat16)
    return pl.pallas_call(
        functools.partial(encode_kernel, lo, hi, tagged, halves),
        out_shape=(out, out),
        in_specs=[HBM] * 3,
        out_specs=[VMEM] * 2,
        scratch_shapes=[
            pltpu.SMEM(flags.shape, jnp.int32),
            pltpu.SMEM((experts, block_cols * block_rows + 1), jnp.int32),
            pltpu.VMEM((experts, BLK, ranks * BLK), jnp.float32),
            pltpu.VMEM((experts, BLK, ranks * BLK), jnp.bfloat16),
            pltpu.SemaphoreType.DMA,
            pltpu.SemaphoreType.DMA((experts, ranks)),
            pltpu.SemaphoreType.DMA((experts, ranks)),
        ],
        compiler_params=params(24),
        cost_estimate=cost(4_000_000_000, 4_000_000),
        name="encode",
    )(*(pltpu.with_memory_space_constraint(a, pltpu.MemorySpace.HBM) for a in (flags, trained, snapshot)))


def by_slot_kernel(placement, own, got, *outs):
    experts = own.shape[0]
    core, expert = axis("replica"), axis("expert")
    for k, out in enumerate(outs):
        chosen = placement[expert ^ k]
        here, at = chosen // experts == core, chosen % experts

        @pl.when(here)
        def _(out=out, at=at):
            out[...] = own[at]

        @pl.when(jnp.logical_not(here))
        def _(out=out, at=at):
            out[...] = got[at]


def by_slot(placement, own, got, count):
    out = jax.ShapeDtypeStruct(own.shape[1:], own.dtype)
    return pl.pallas_call(
        by_slot_kernel,
        out_shape=(out,) * count,
        in_specs=[SMEM, VMEM, VMEM],
        out_specs=[VMEM] * count,
        compiler_params=params(16),
        cost_estimate=cost(1_000_000_000, 2_000_000),
        name="by_slot",
    )(placement, own, got)


def by_range_kernel(members, count, held, *refs):
    pieces, kept, outs = refs[:count], refs[count : count + held], refs[count + held :]
    rows = pieces[0].shape[0]
    shift = axis("expert") ^ (axis("tensor") * members)
    for j in range(held):
        before = kept[j].shape[0] // members
        for u in range(members):
            outs[j][pl.ds(u * (before + rows), before), :] = kept[j][pl.ds(u * before, before), :]
    for case in range(count):

        @pl.when(shift == case)
        def _(case=case):
            for j, out in enumerate(outs):
                each = out.shape[0] // members
                for u in range(members):
                    out[pl.ds(u * each + each - rows, rows), :] = pieces[case ^ (j * members + u)][...]


def by_range(pieces, kept, members):
    rows, cols = pieces[0].shape
    total, count = len(pieces) // members, len(pieces)
    outs = []
    for j in range(total):
        before = kept[j].shape[0] if j < len(kept) else 0
        outs.append(jax.ShapeDtypeStruct((members * rows + before, cols), pieces[0].dtype))
    return pl.pallas_call(
        functools.partial(by_range_kernel, members, count, len(kept)),
        out_shape=outs,
        in_specs=[VMEM] * (count + len(kept)),
        out_specs=[VMEM] * total,
        compiler_params=params(16),
        cost_estimate=cost(1_000_000_000, 2_000_000),
        name="by_range",
    )(*pieces, *kept)


def clear_kernel(out, zeros, sems):
    zeros[...] = jnp.zeros_like(zeros)
    step = zeros.shape[0]

    def blank(i):
        return pltpu.make_async_copy(zeros, out.at[0, pl.ds(i * step, step), :], sems.at[i])

    for i in range(out.shape[1] // step):
        blank(i).start()
    for i in range(out.shape[1] // step):
        blank(i).wait()


def clear(shape, step):
    return pl.pallas_call(
        clear_kernel,
        out_shape=jax.ShapeDtypeStruct(shape, jnp.bfloat16),
        out_specs=HBM,
        scratch_shapes=[pltpu.VMEM((step, shape[2]), jnp.bfloat16), pltpu.SemaphoreType.DMA((shape[1] // step,))],
        compiler_params=params(4),
        cost_estimate=cost(2_000_000_000, 7_000_000),
        name="clear",
    )()


def place_kernel(turns, lines, members, lo, ranks, gap, block_cols, local_rows, local_cols, tags, *refs):
    count = len(turns)
    mine, theirs = refs[:count], refs[count : 2 * count]
    out, sems = refs[-2:]
    part = BLK // 2
    rows_each = mine[0].shape[0] // members
    own_row = axis("replica") * part
    tensor = axis("tensor")
    spans = []
    for i, turn in enumerate(turns):
        for u in range(members):
            line = lines[i] * members + u
            found = jnp.clip(tags[line, BLK - 1] - lo, 0, ranks)
            spans.append((i, u, found))

            @pl.loop(0, found)
            def _(j, i=i, u=u, turn=turn, line=line):
                spot = tags[line, lo + j]
                row = (tensor ^ turn) * local_rows + (spot // block_cols) * BLK
                cols = pl.ds(pl.multiple_of(u * local_cols + (spot % block_cols) * BLK, BLK), BLK)
                skip = jnp.where(j >= gap, TAG_ROWS, 0)
                source = pl.ds(pl.multiple_of(u * rows_each + j * part + skip, TAG_ROWS), part)
                for k, (held, start) in enumerate(((mine[i], own_row), (theirs[i], part - own_row))):
                    target = out.at[0, pl.ds(pl.multiple_of(row + start, part), part), cols]
                    pltpu.make_async_copy(held.at[source, :], target, sems.at[k, i * members + u, j]).start()

    for i, u, found in spans:

        @pl.loop(0, found)
        def _(j, i=i, u=u):
            for k, held in enumerate((mine[i], theirs[i])):
                target = out.at[0, pl.ds(0, part), pl.ds(0, BLK)]
                pltpu.make_async_copy(held.at[pl.ds(0, part), :], target, sems.at[k, i * members + u, j]).wait()


def place(out, tags, mine, theirs, turns, lines, members, lo, ranks, gap, sizes):
    count = len(turns)
    return pl.pallas_call(
        functools.partial(place_kernel, turns, lines, members, lo, ranks, gap, *sizes),
        out_shape=jax.ShapeDtypeStruct(out.shape, out.dtype),
        in_specs=[SMEM] + [VMEM] * (2 * count) + [HBM],
        out_specs=HBM,
        scratch_shapes=[pltpu.SemaphoreType.DMA((2, count * members, ranks))],
        input_output_aliases={1 + 2 * count: 0},
        compiler_params=params(16),
        cost_estimate=cost(2_000_000_000, 4_000_000),
        name="place",
    )(tags, *mine, *theirs, out)


def push(trained, snapshot, changed, placement):
    _, local_rows, local_cols = trained.shape
    copies = lax.axis_size("replica")
    tensor_count = lax.axis_size("tensor")
    expert_count = lax.axis_size("expert")
    members = expert_count // tensor_count
    block_rows, block_cols = local_rows // BLK, local_cols // BLK
    block_count = block_rows * block_cols
    capacity = (4 * block_count + 3) // 7
    axes = ("expert", "tensor", "replica")

    def device(e, t, r):
        return (e * tensor_count + t) * copies + r

    def permute(array, target):
        pairs = [
            (device(e, t, r), device(*target(e, t, r)))
            for e in range(expert_count)
            for t in range(tensor_count)
            for r in range(copies)
        ]
        return lax.ppermute(array, axes, pairs)

    def swap(e, t, r):
        return e, t, 1 - r

    flags = jnp.transpose(changed, (0, 2, 1))
    part = BLK // copies
    first = max(1, capacity * 3 // 8)
    rounds = [(0, first), (first, capacity)]
    near, far = [0], list(range(2, tensor_count)) + [1]
    sizes = (block_cols, local_rows, local_cols)
    out = clear((1, tensor_count * local_rows, members * local_cols), 256)

    def taken(pieces):
        lines = [p[u * (p.shape[0] // members) + first * part] for p in pieces for u in range(members)]
        return jnp.stack(lines).astype(jnp.int32)

    kept = []
    for i, (lo, hi) in enumerate(rounds):
        own, oth = encode(trained, snapshot, flags, lo, hi, i == 0, copies)
        got = permute(oth, swap)
        pieces = list(by_slot(placement, own, got, expert_count))
        for k in range(1, expert_count):
            pieces[k] = permute(pieces[k], lambda e, t, r: (e ^ k, t, r))
        pieces = list(by_range(pieces, kept, members))
        kept = pieces[: len(near)]
        for j in far:
            pieces[j] = permute(pieces[j], lambda e, t, r: (e, t ^ j, r))
        theirs = {j: permute(pieces[j], swap) for j in far}
        if i == 0:
            tags = taken([theirs[j] for j in sorted(far)])
        else:
            theirs.update({j: permute(kept[j], swap) for j in near})
            pair = [theirs[j] for j in near]
            out = place(out, taken(pair), kept, pair, near, near, members, 0, capacity, first, sizes)
        for group in [[j] for j in far[::-1]] if i else [sorted(far)]:
            out = place(
                out,
                tags,
                [pieces[j] for j in group],
                [theirs[j] for j in group],
                group,
                [j - len(near) for j in group],
                members,
                lo,
                hi - lo,
                hi - lo,
                sizes,
            )
    return out


def solution(mesh):
    split = P("replica", "tensor", "expert")
    return jax.shard_map(
        push,
        mesh=mesh,
        in_specs=(split, split, split, P()),
        out_specs=P("expert", None, "tensor"),
        check_vma=False,
    )
```

time: 96.5 us -> 84.6 us (0.88)
  waiting for transfers between devices: 58.2 us -> 38.9 us
  starting transfers between devices: 19.4 us -> 24.2 us
  Pallas kernels: 17.9 us -> 20.9 us
    ppermute x22 -> x21, waiting for transfers between devices: 58.2 us -> 38.9 us  [permute(): return lax.ppermute(array, axes, pairs)]
    ppermute x22 -> x21, starting transfers between devices: 19.4 us -> 24.2 us  [permute(): return lax.ppermute(array, axes, pairs)]
    pallas_call x7 -> x9, Pallas kernels: 13.3 us -> 16.3 us  [the longest x5 9.14 us: place(): pl.pallas_call(functools.partial(place_kernel, turns, lines, members, lo,...]
  transfers between devices with their start and end apart: 22 -> 21, of which waited for: 8 -> 9; matrix products, arithmetic and copies ran while one was open for 0% -> 0% of each run, Pallas kernels for 12% -> 19%
where the time goes in v2:
time: 84.6 us; the launch traced here: 84.3 us
  waiting for transfers between devices  38.9 us (46%)
  starting transfers between devices  24.2 us (29%)
  Pallas kernels  20.9 us (25%)
    ppermute x21, waiting for transfers between devices, permute(): return lax.ppermute(array, axes, pairs)  38.9 us
    ppermute x21, starting transfers between devices, permute(): return lax.ppermute(array, axes, pairs)  24.2 us
    pallas_call x5, Pallas kernels, place(): pl.pallas_call(functools.partial(place_kernel, turns, lines, members, lo,...  9.14 us
    pallas_call x2, Pallas kernels, encode(): pl.pallas_call(functools.partial(encode_kernel, lo, hi, tagged, halves),...  7.01 us
    pallas_call x1, Pallas kernels, clear(): pl.pallas_call(clear_kernel, out_shape=jax.ShapeDtypeStruct(shape, jnp.bf...  3.21 us
  transfers between devices with their start and end apart: 21, of which 9 were waited for; matrix products, arithmetic and copies ran while one was open for 0% of the time, Pallas kernels for 19%

profile of v2, /device:TPU:0, one launch (start us, length us, event | category | flops | bytes accessed | tf_op | source)
XLA Modules:
  0.0 84.3 jit_solution(6196135998251466046)
XLA Ops:
  0.0 3.7 %encode.3 = (bf16[2,1280,128]{2,1,0:T(8,128)(2,1)S(1)}, bf16[2,1280,128]{2,1,0:T(8,128)(2,1)S(1)}) custom-call(s32[2,4,14]{2,1,0:T(4,128)} %bitcast.1, f32[2,1792,512]{2,1,0:T(8,128)} %new_hbm.3, bf16[2,1792,512]{2,1,0:T(8,128)(2,1)} %old_hbm.3), custom_call_target="tpu_custom_call" | custom-call | flops 4000000000 | bytes 4000000 | tf_op jit(solution)/shard_map/encode/pallas_call | solution.py:107
  3.7 0.7 collective-permute-start.10
  4.5 3.3 %encode.2 = (bf16[2,784,128]{2,1,0:T(8,128)(2,1)S(1)}, bf16[2,784,128]{2,1,0:T(8,128)(2,1)S(1)}) custom-call(s32[2,4,14]{2,1,0:T(4,128)} %bitcast.2, f32[2,1792,512]{2,1,0:T(8,128)} %new_hbm.3, bf16[2,1792,512]{2,1,0:T(8,128)(2,1)} %old_hbm.3), custom_call_target="tpu_custom_call" | custom-call | flops 4000000000 | bytes 4000000 | tf_op jit(solution)/shard_map/encode/pallas_call | solution.py:107
  8.0 1.6 %collective-permute-done.got = bf16[2,784,128]{2,1,0:T(8,128)(2,1)S(1)} collective-permute-done((bf16[2,784,128]{2,1,0:T(8,128)(2,1)S(1)}, bf16[2,784,128]{2,1,0:T(8,128)(2,1)S(1)}, u32[]{:S(2)}, u32[]{:S(2)}) %collective-permute-start) | collective-permute-done | bytes 401440 | tf_op jit(solution)/shard_map/ppermute | solution.py:288
  9.6 0.7 by_slot.2
  10.3 1.6 %collective-permute-start.1 = (bf16[784,128]{1,0:T(8,128)(2,1)S(1)}, bf16[784,128]{1,0:T(8,128)(2,1)S(1)}, u32[]{:S(2)}, u32[]{:S(2)}) collective-permute-start(bf16[784,128]{1,0:T(8,128)(2,1)S(1)} %get-tuple-element.28), channel_id=1, source_target_pairs={{0,8},{1,9},{2,10},{3,11},{4,12},{5,13},{6,14},{7,15},{8,0},{9,1},... | collective-permute-start | bytes 602120 | tf_op jit(solution)/shard_map/ppermute | solution.py:288
  11.9 1.5 %collective-permute-start.2 = (bf16[784,128]{1,0:T(8,128)(2,1)S(1)}, bf16[784,128]{1,0:T(8,128)(2,1)S(1)}, u32[]{:S(2)}, u32[]{:S(2)}) collective-permute-start(bf16[784,128]{1,0:T(8,128)(2,1)S(1)} %get-tuple-element.29), channel_id=1, source_target_pairs={{0,16},{1,17},{2,18},{3,19},{4,20},{5,21},{6,22},{7,23},{8,24},{9,... | collective-permute-start | bytes 602120 | tf_op jit(solution)/shard_map/ppermute | solution.py:288
  13.4 1.4 %collective-permute-start.3 = (bf16[784,128]{1,0:T(8,128)(2,1)S(1)}, bf16[784,128]{1,0:T(8,128)(2,1)S(1)}, u32[]{:S(2)}, u32[]{:S(2)}) collective-permute-start(bf16[784,128]{1,0:T(8,128)(2,1)S(1)} %get-tuple-element.30), channel_id=1, source_target_pairs={{0,24},{1,25},{2,26},{3,27},{4,28},{5,29},{6,30},{7,31},{8,16},{9,... | collective-permute-start | bytes 602120 | tf_op jit(solution)/shard_map/ppermute | solution.py:288
  14.8 0.7 by_slot.3
  15.5 0.7 collective-permute-start.11
  16.2 1.5 %collective-permute-start.12 = (bf16[1280,128]{1,0:T(8,128)(2,1)S(1)}, bf16[1280,128]{1,0:T(8,128)(2,1)S(1)}, u32[]{:S(2)}, u32[]{:S(2)}) collective-permute-start(bf16[1280,128]{1,0:T(8,128)(2,1)S(1)} %get-tuple-element.38), channel_id=1, source_target_pairs={{0,16},{1,17},{2,18},{3,19},{4,20},{5,21},{6,22},{7,23},{8,24},{9,... | collective-permute-start | bytes 983048 | tf_op jit(solution)/shard_map/ppermute | solution.py:288
  17.7 0.5 collective-permute-done.1.refs_1_
  18.2 2.5 %collective-permute-start.13 = (bf16[1280,128]{1,0:T(8,128)(2,1)S(1)}, bf16[1280,128]{1,0:T(8,128)(2,1)S(1)}, u32[]{:S(2)}, u32[]{:S(2)}) collective-permute-start(bf16[1280,128]{1,0:T(8,128)(2,1)S(1)} %get-tuple-element.39), channel_id=1, source_target_pairs={{0,24},{1,25},{2,26},{3,27},{4,28},{5,29},{6,30},{7,31},{8,16},{9,... | collective-permute-start | bytes 983048 | tf_op jit(solution)/shard_map/ppermute | solution.py:288
  20.6 2.5 %collective-permute-done.2.refs_2_ = bf16[784,128]{1,0:T(8,128)(2,1)S(1)} collective-permute-done((bf16[784,128]{1,0:T(8,128)(2,1)S(1)}, bf16[784,128]{1,0:T(8,128)(2,1)S(1)}, u32[]{:S(2)}, u32[]{:S(2)}) %collective-permute-start.2) | collective-permute-done | bytes 200736 | tf_op jit(solution)/shard_map/ppermute | solution.py:288
  23.1 1.9 %collective-permute-done.3.refs_3_ = bf16[784,128]{1,0:T(8,128)(2,1)S(1)} collective-permute-done((bf16[784,128]{1,0:T(8,128)(2,1)S(1)}, bf16[784,128]{1,0:T(8,128)(2,1)S(1)}, u32[]{:S(2)}, u32[]{:S(2)}) %collective-permute-start.3) | collective-permute-done | bytes 200736 | tf_op jit(solution)/shard_map/ppermute | solution.py:288
  25.1 2.1 %collective-permute-start.4 = (bf16[784,128]{1,0:T(8,128)(2,1)S(1)}, bf16[784,128]{1,0:T(8,128)(2,1)S(1)}, u32[]{:S(2)}, u32[]{:S(2)}) collective-permute-start(bf16[784,128]{1,0:T(8,128)(2,1)S(1)} %get-tuple-element.31), channel_id=1, source_target_pairs={{0,2},{1,3},{2,0},{3,1},{4,6},{5,7},{6,4},{7,5},{8,10},{9,11},{10,... | collective-permute-start | bytes 602120 | tf_op jit(solution)/shard_map/ppermute | solution.py:288
  27.2 2.2 %collective-permute-start.6 = (bf16[784,128]{1,0:T(8,128)(2,1)S(1)}, bf16[784,128]{1,0:T(8,128)(2,1)S(1)}, u32[]{:S(2)}, u32[]{:S(2)}) collective-permute-start(bf16[784,128]{1,0:T(8,128)(2,1)S(1)} %get-tuple-element.32), channel_id=1, source_target_pairs={{0,4},{1,5},{2,6},{3,7},{4,0},{5,1},{6,2},{7,3},{8,12},{9,13},{10,... | collective-permute-start | bytes 602120 | tf_op jit(solution)/shard_map/ppermute | solution.py:288
  29.4 5.0 %collective-permute-done.4.refs_0_ = bf16[784,128]{1,0:T(8,128)(2,1)S(1)} collective-permute-done((bf16[784,128]{1,0:T(8,128)(2,1)S(1)}, bf16[784,128]{1,0:T(8,128)(2,1)S(1)}, u32[]{:S(2)}, u32[]{:S(2)}) %collective-permute-start.4) | collective-permute-done | bytes 200736 | tf_op jit(solution)/shard_map/ppermute | solution.py:288
  34.4 3.3 %collective-permute-start.8 = (bf16[784,128]{1,0:T(8,128)(2,1)S(1)}, bf16[784,128]{1,0:T(8,128)(2,1)S(1)}, u32[]{:S(2)}, u32[]{:S(2)}) collective-permute-start(bf16[784,128]{1,0:T(8,128)(2,1)S(1)} %get-tuple-element.33), channel_id=1, source_target_pairs={{0,6},{1,7},{2,4},{3,5},{4,2},{5,3},{6,0},{7,1},{8,14},{9,15},{10,... | collective-permute-start | bytes 602120 | tf_op jit(solution)/shard_map/ppermute | solution.py:288
  37.7 5.1 %collective-permute-done.6.refs_1_ = bf16[784,128]{1,0:T(8,128)(2,1)S(1)} collective-permute-done((bf16[784,128]{1,0:T(8,128)(2,1)S(1)}, bf16[784,128]{1,0:T(8,128)(2,1)S(1)}, u32[]{:S(2)}, u32[]{:S(2)}) %collective-permute-start.6) | collective-permute-done | bytes 200736 | tf_op jit(solution)/shard_map/ppermute | solution.py:288
  42.8 0.5 collective-permute-start.7
  43.5 0.5 collective-permute-start.9
  44.0 2.9 %collective-permute-start.18 = (bf16[1280,128]{1,0:T(8,128)(2,1)S(1)}, bf16[1280,128]{1,0:T(8,128)(2,1)S(1)}, u32[]{:S(2)}, u32[]{:S(2)}) collective-permute-start(bf16[1280,128]{1,0:T(8,128)(2,1)S(1)} %get-tuple-element.43), channel_id=1, source_target_pairs={{0,2},{1,3},{2,0},{3,1},{4,6},{5,7},{6,4},{7,5},{8,10},{9,11},{10,... | collective-permute-start | bytes 983048 | tf_op jit(solution)/shard_map/ppermute | solution.py:288
  46.9 2.5 %collective-permute-start.16 = (bf16[1280,128]{1,0:T(8,128)(2,1)S(1)}, bf16[1280,128]{1,0:T(8,128)(2,1)S(1)}, u32[]{:S(2)}, u32[]{:S(2)}) collective-permute-start(bf16[1280,128]{1,0:T(8,128)(2,1)S(1)} %get-tuple-element.42), channel_id=1, source_target_pairs={{0,6},{1,7},{2,4},{3,5},{4,2},{5,3},{6,0},{7,1},{8,14},{9,15},{10,... | collective-permute-start | bytes 983048 | tf_op jit(solution)/shard_map/ppermute | solution.py:288
  49.4 3.2 %clear.1.refs_6_ = bf16[1,7168,512]{2,1,0:T(8,128)(2,1)} custom-call(), custom_call_target="tpu_custom_call" | custom-call | flops 2000000000 | bytes 7000000 | tf_op jit(solution)/shard_map/clear/pallas_call | solution.py:206
  52.7 2.5 %place.5.refs_2_ = bf16[1,7168,512]{2,1,0:T(8,128)(2,1)} custom-call(s32[3,128]{1,0:T(4,128)S(1)} %maximum_convert_fusion.tags, bf16[784,128]{1,0:T(8,128)(2,1)S(1)} %collective-permute-done.4.refs_0_, bf16[784,128]{1,0:T(8,128)(2,1)S(1)} %collective-permute-done.6.refs_1_, ...), custom_call_target="tpu_custom_call", output_to_operand_aliasing={{}: (7, {})} | custom-call | flops 2000000000 | bytes 4000000 | tf_op jit(solution)/shard_map/place/pallas_call | solution.py:254
  55.3 9.8 %collective-permute-done.16.refs_0_ = bf16[1280,128]{1,0:T(8,128)(2,1)S(1)} collective-permute-done((bf16[1280,128]{1,0:T(8,128)(2,1)S(1)}, bf16[1280,128]{1,0:T(8,128)(2,1)S(1)}, u32[]{:S(2)}, u32[]{:S(2)}) %collective-permute-start.16) | collective-permute-done | bytes 327712 | tf_op jit(solution)/shard_map/ppermute | solution.py:288
  65.1 12.4 %collective-permute-done.14.refs_0_ = bf16[1280,128]{1,0:T(8,128)(2,1)S(1)} collective-permute-done((bf16[1280,128]{1,0:T(8,128)(2,1)S(1)}, bf16[1280,128]{1,0:T(8,128)(2,1)S(1)}, u32[]{:S(2)}, u32[]{:S(2)}) %collective-permute-start.14) | collective-permute-done | bytes 327712 | tf_op jit(solution)/shard_map/ppermute | solution.py:288
  77.5 2.2 %place.6.refs_2_ = bf16[1,7168,512]{2,1,0:T(8,128)(2,1)} custom-call(s32[1,128]{1,0:T(1,128)S(1)} %slice_convert_fusion.tags, bf16[2064,128]{1,0:T(8,128)(2,1)S(1)} %get-tuple-element.44.refs_0_, bf16[2064,128]{1,0:T(8,128)(2,1)S(1)} %collective-permute-done.20.refs_1_, bf16[1,7168,512]{2,1,0:T(8,128)(2,1)} %place.5.refs_2_), custom_call_target="tpu_custom_call", output_to_operand_aliasing={{}: (3, {})} | custom-call | flops 2000000000 | bytes 4000000 | tf_op jit(solution)/shard_map/place/pallas_call | solution.py:254
  79.7 2.0 %place.7.refs_2_ = bf16[1,7168,512]{2,1,0:T(8,128)(2,1)} custom-call(s32[3,128]{1,0:T(4,128)S(1)} %maximum_convert_fusion.tags, bf16[1280,128]{1,0:T(8,128)(2,1)S(1)} %collective-permute-done.18.refs_0_, bf16[1280,128]{1,0:T(8,128)(2,1)S(1)} %collective-permute-done.19.refs_1_, bf16[1,7168,512]{2,1,0:T(8,128)(2,1)} %place.6.refs_2_), custom_call_target="tpu_custom_call", output_to_operand_aliasing={{}: (3, {})} | custom-call | flops 2000000000 | bytes 4000000 | tf_op jit(solution)/shard_map/place/pallas_call | solution.py:254
  81.7 1.6 %place.8.refs_2_ = bf16[1,7168,512]{2,1,0:T(8,128)(2,1)} custom-call(s32[3,128]{1,0:T(4,128)S(1)} %maximum_convert_fusion.tags, bf16[1280,128]{1,0:T(8,128)(2,1)S(1)} %collective-permute-done.16.refs_0_, bf16[1280,128]{1,0:T(8,128)(2,1)S(1)} %collective-permute-done.17.refs_1_, bf16[1,7168,512]{2,1,0:T(8,128)(2,1)} %place.7.refs_2_), custom_call_target="tpu_custom_call", output_to_operand_aliasing={{}: (3, {})} | custom-call | flops 2000000000 | bytes 4000000 | tf_op jit(solution)/shard_map/place/pallas_call | solution.py:254
  83.3 0.9 %place.9 = bf16[1,7168,512]{2,1,0:T(8,128)(2,1)} custom-call(s32[3,128]{1,0:T(4,128)S(1)} %maximum_convert_fusion.tags, bf16[1280,128]{1,0:T(8,128)(2,1)S(1)} %collective-permute-done.14.refs_0_, bf16[1280,128]{1,0:T(8,128)(2,1)S(1)} %collective-permute-done.15.refs_1_, bf16[1,7168,512]{2,1,0:T(8,128)(2,1)} %place.8.refs_2_), custom_call_target="tpu_custom_call", output_to_operand_aliasing={{}: (3, {})} | custom-call | flops 2000000000 | bytes 4000000 | tf_op jit(solution)/shard_map/place/pallas_call | solution.py:254
  (29 shorter events, 0.7 us)
Async XLA Ops:
  3.7 5.9 %copy-start = (s32[4]{0:T(128)S(1)}, s32[4]{0:T(128)}, u32[]{:S(2)}) copy-start(s32[4]{0:T(128)} %placement.3) | copy-start | bytes 52
  3.7 11.1 %collective-permute-start.10 = (bf16[2,1280,128]{2,1,0:T(8,128)(2,1)S(1)}, bf16[2,1280,128]{2,1,0:T(8,128)(2,1)S(1)}, u32[]{:S(2)}, u32[]{:S(2)}) collective-permute-start(bf16[2,1280,128]{2,1,0:T(8,128)(2,1)S(1)} %get-tuple-element.35), channel_id=1, source_target_pairs={{0,1},{1,0},{2,3},{3,2},{4,5},{5,4},{6,7},{7,6},{8,9},{9,8},{10,11... | collective-permute-start | bytes 1966088 | tf_op jit(solution)/shard_map/ppermute | solution.py:288
  7.8 1.8 %collective-permute-start = (bf16[2,784,128]{2,1,0:T(8,128)(2,1)S(1)}, bf16[2,784,128]{2,1,0:T(8,128)(2,1)S(1)}, u32[]{:S(2)}, u32[]{:S(2)}) collective-permute-start(bf16[2,784,128]{2,1,0:T(8,128)(2,1)S(1)} %get-tuple-element.26), channel_id=1, source_target_pairs={{0,1},{1,0},{2,3},{3,2},{4,5},{5,4},{6,7},{7,6},{8,9},{9,8},{10,11... | collective-permute-start | bytes 1204232 | tf_op jit(solution)/shard_map/ppermute | solution.py:288
  10.3 7.9 %collective-permute-start.1 = (bf16[784,128]{1,0:T(8,128)(2,1)S(1)}, bf16[784,128]{1,0:T(8,128)(2,1)S(1)}, u32[]{:S(2)}, u32[]{:S(2)}) collective-permute-start(bf16[784,128]{1,0:T(8,128)(2,1)S(1)} %get-tuple-element.28), channel_id=1, source_target_pairs={{0,8},{1,9},{2,10},{3,11},{4,12},{5,13},{6,14},{7,15},{8,0},{9,1},... | collective-permute-start | bytes 602120 | tf_op jit(solution)/shard_map/ppermute | solution.py:288
  11.9 11.2 %collective-permute-start.2 = (bf16[784,128]{1,0:T(8,128)(2,1)S(1)}, bf16[784,128]{1,0:T(8,128)(2,1)S(1)}, u32[]{:S(2)}, u32[]{:S(2)}) collective-permute-start(bf16[784,128]{1,0:T(8,128)(2,1)S(1)} %get-tuple-element.29), channel_id=1, source_target_pairs={{0,16},{1,17},{2,18},{3,19},{4,20},{5,21},{6,22},{7,23},{8,24},{9,... | collective-permute-start | bytes 602120 | tf_op jit(solution)/shard_map/ppermute | solution.py:288
  13.4 11.6 %collective-permute-start.3 = (bf16[784,128]{1,0:T(8,128)(2,1)S(1)}, bf16[784,128]{1,0:T(8,128)(2,1)S(1)}, u32[]{:S(2)}, u32[]{:S(2)}) collective-permute-start(bf16[784,128]{1,0:T(8,128)(2,1)S(1)} %get-tuple-element.30), channel_id=1, source_target_pairs={{0,24},{1,25},{2,26},{3,27},{4,28},{5,29},{6,30},{7,31},{8,16},{9,... | collective-permute-start | bytes 602120 | tf_op jit(solution)/shard_map/ppermute | solution.py:288
  15.5 27.3 %collective-permute-start.11 = (bf16[1280,128]{1,0:T(8,128)(2,1)S(1)}, bf16[1280,128]{1,0:T(8,128)(2,1)S(1)}, u32[]{:S(2)}, u32[]{:S(2)}) collective-permute-start(bf16[1280,128]{1,0:T(8,128)(2,1)S(1)} %get-tuple-element.37), channel_id=1, source_target_pairs={{0,8},{1,9},{2,10},{3,11},{4,12},{5,13},{6,14},{7,15},{8,0},{9,1},... | collective-permute-start | bytes 983048 | tf_op jit(solution)/shard_map/ppermute | solution.py:288
  16.2 27.1 %collective-permute-start.12 = (bf16[1280,128]{1,0:T(8,128)(2,1)S(1)}, bf16[1280,128]{1,0:T(8,128)(2,1)S(1)}, u32[]{:S(2)}, u32[]{:S(2)}) collective-permute-start(bf16[1280,128]{1,0:T(8,128)(2,1)S(1)} %get-tuple-element.38), channel_id=1, source_target_pairs={{0,16},{1,17},{2,18},{3,19},{4,20},{5,21},{6,22},{7,23},{8,24},{9,... | collective-permute-start | bytes 983048 | tf_op jit(solution)/shard_map/ppermute | solution.py:288
  18.2 25.1 %collective-permute-start.13 = (bf16[1280,128]{1,0:T(8,128)(2,1)S(1)}, bf16[1280,128]{1,0:T(8,128)(2,1)S(1)}, u32[]{:S(2)}, u32[]{:S(2)}) collective-permute-start(bf16[1280,128]{1,0:T(8,128)(2,1)S(1)} %get-tuple-element.39), channel_id=1, source_target_pairs={{0,24},{1,25},{2,26},{3,27},{4,28},{5,29},{6,30},{7,31},{8,16},{9,... | collective-permute-start | bytes 983048 | tf_op jit(solution)/shard_map/ppermute | solution.py:288
  25.1 9.3 %collective-permute-start.4 = (bf16[784,128]{1,0:T(8,128)(2,1)S(1)}, bf16[784,128]{1,0:T(8,128)(2,1)S(1)}, u32[]{:S(2)}, u32[]{:S(2)}) collective-permute-start(bf16[784,128]{1,0:T(8,128)(2,1)S(1)} %get-tuple-element.31), channel_id=1, source_target_pairs={{0,2},{1,3},{2,0},{3,1},{4,6},{5,7},{6,4},{7,5},{8,10},{9,11},{10,... | collective-permute-start | bytes 602120 | tf_op jit(solution)/shard_map/ppermute | solution.py:288
  27.2 15.6 %collective-permute-start.6 = (bf16[784,128]{1,0:T(8,128)(2,1)S(1)}, bf16[784,128]{1,0:T(8,128)(2,1)S(1)}, u32[]{:S(2)}, u32[]{:S(2)}) collective-permute-start(bf16[784,128]{1,0:T(8,128)(2,1)S(1)} %get-tuple-element.32), channel_id=1, source_target_pairs={{0,4},{1,5},{2,6},{3,7},{4,0},{5,1},{6,2},{7,3},{8,12},{9,13},{10,... | collective-permute-start | bytes 602120 | tf_op jit(solution)/shard_map/ppermute | solution.py:288
  34.4 9.1 %collective-permute-start.8 = (bf16[784,128]{1,0:T(8,128)(2,1)S(1)}, bf16[784,128]{1,0:T(8,128)(2,1)S(1)}, u32[]{:S(2)}, u32[]{:S(2)}) collective-permute-start(bf16[784,128]{1,0:T(8,128)(2,1)S(1)} %get-tuple-element.33), channel_id=1, source_target_pairs={{0,6},{1,7},{2,4},{3,5},{4,2},{5,3},{6,0},{7,1},{8,14},{9,15},{10,... | collective-permute-start | bytes 602120 | tf_op jit(solution)/shard_map/ppermute | solution.py:288
  42.8 4.1 %collective-permute-start.5 = (bf16[784,128]{1,0:T(8,128)(2,1)S(1)}, bf16[784,128]{1,0:T(8,128)(2,1)S(1)}, u32[]{:S(2)}, u32[]{:S(2)}) collective-permute-start(bf16[784,128]{1,0:T(8,128)(2,1)S(1)} %collective-permute-done.4.refs_0_), channel_id=1, source_target_pairs={{0,1},{1,0},{2,3},{3,2},{4,5},{5,4},{6,7},{7,6},{8,9},{9,8},{10,11... | collective-permute-start | bytes 602120 | tf_op jit(solution)/shard_map/ppermute | solution.py:288
  42.8 6.6 %collective-permute-start.7 = (bf16[784,128]{1,0:T(8,128)(2,1)S(1)}, bf16[784,128]{1,0:T(8,128)(2,1)S(1)}, u32[]{:S(2)}, u32[]{:S(2)}) collective-permute-start(bf16[784,128]{1,0:T(8,128)(2,1)S(1)} %collective-permute-done.6.refs_1_), channel_id=1, source_target_pairs={{0,1},{1,0},{2,3},{3,2},{4,5},{5,4},{6,7},{7,6},{8,9},{9,8},{10,11... | collective-permute-start | bytes 602120 | tf_op jit(solution)/shard_map/ppermute | solution.py:288
  43.4 34.1 %collective-permute-start.20 = (bf16[2064,128]{1,0:T(8,128)(2,1)S(1)}, bf16[2064,128]{1,0:T(8,128)(2,1)S(1)}, u32[]{:S(2)}, u32[]{:S(2)}) collective-permute-start(bf16[2064,128]{1,0:T(8,128)(2,1)S(1)} %get-tuple-element.44.refs_0_), channel_id=1, source_target_pairs={{0,1},{1,0},{2,3},{3,2},{4,5},{5,4},{6,7},{7,6},{8,9},{9,8},{10,11... | collective-permute-start | bytes 1585160 | tf_op jit(solution)/shard_map/ppermute | solution.py:288
  43.5 9.1 %collective-permute-start.9 = (bf16[784,128]{1,0:T(8,128)(2,1)S(1)}, bf16[784,128]{1,0:T(8,128)(2,1)S(1)}, u32[]{:S(2)}, u32[]{:S(2)}) collective-permute-start(bf16[784,128]{1,0:T(8,128)(2,1)S(1)} %collective-permute-done.8.refs_2_), channel_id=1, source_target_pairs={{0,1},{1,0},{2,3},{3,2},{4,5},{5,4},{6,7},{7,6},{8,9},{9,8},{10,11... | collective-permute-start | bytes 602120 | tf_op jit(solution)/shard_map/ppermute | solution.py:288
  44.0 11.2 %collective-permute-start.18 = (bf16[1280,128]{1,0:T(8,128)(2,1)S(1)}, bf16[1280,128]{1,0:T(8,128)(2,1)S(1)}, u32[]{:S(2)}, u32[]{:S(2)}) collective-permute-start(bf16[1280,128]{1,0:T(8,128)(2,1)S(1)} %get-tuple-element.43), channel_id=1, source_target_pairs={{0,2},{1,3},{2,0},{3,1},{4,6},{5,7},{6,4},{7,5},{8,10},{9,11},{10,... | collective-permute-start | bytes 983048 | tf_op jit(solution)/shard_map/ppermute | solution.py:288
  46.9 18.2 %collective-permute-start.16 = (bf16[1280,128]{1,0:T(8,128)(2,1)S(1)}, bf16[1280,128]{1,0:T(8,128)(2,1)S(1)}, u32[]{:S(2)}, u32[]{:S(2)}) collective-permute-start(bf16[1280,128]{1,0:T(8,128)(2,1)S(1)} %get-tuple-element.42), channel_id=1, source_target_pairs={{0,6},{1,7},{2,4},{3,5},{4,2},{5,3},{6,0},{7,1},{8,14},{9,15},{10,... | collective-permute-start | bytes 983048 | tf_op jit(solution)/shard_map/ppermute | solution.py:288
  49.4 28.1 %collective-permute-start.14 = (bf16[1280,128]{1,0:T(8,128)(2,1)S(1)}, bf16[1280,128]{1,0:T(8,128)(2,1)S(1)}, u32[]{:S(2)}, u32[]{:S(2)}) collective-permute-start(bf16[1280,128]{1,0:T(8,128)(2,1)S(1)} %get-tuple-element.41), channel_id=1, source_target_pairs={{0,4},{1,5},{2,6},{3,7},{4,0},{5,1},{6,2},{7,3},{8,12},{9,13},{10,... | collective-permute-start | bytes 983048 | tf_op jit(solution)/shard_map/ppermute | solution.py:288
  55.2 24.4 %collective-permute-start.19 = (bf16[1280,128]{1,0:T(8,128)(2,1)S(1)}, bf16[1280,128]{1,0:T(8,128)(2,1)S(1)}, u32[]{:S(2)}, u32[]{:S(2)}) collective-permute-start(bf16[1280,128]{1,0:T(8,128)(2,1)S(1)} %collective-permute-done.18.refs_0_), channel_id=1, source_target_pairs={{0,1},{1,0},{2,3},{3,2},{4,5},{5,4},{6,7},{7,6},{8,9},{9,8},{10,11... | collective-permute-start | bytes 983048 | tf_op jit(solution)/shard_map/ppermute | solution.py:288
  65.1 16.6 %collective-permute-start.17 = (bf16[1280,128]{1,0:T(8,128)(2,1)S(1)}, bf16[1280,128]{1,0:T(8,128)(2,1)S(1)}, u32[]{:S(2)}, u32[]{:S(2)}) collective-permute-start(bf16[1280,128]{1,0:T(8,128)(2,1)S(1)} %collective-permute-done.16.refs_0_), channel_id=1, source_target_pairs={{0,1},{1,0},{2,3},{3,2},{4,5},{5,4},{6,7},{7,6},{8,9},{9,8},{10,11... | collective-permute-start | bytes 983048 | tf_op jit(solution)/shard_map/ppermute | solution.py:288
  77.5 5.8 %collective-permute-start.15 = (bf16[1280,128]{1,0:T(8,128)(2,1)S(1)}, bf16[1280,128]{1,0:T(8,128)(2,1)S(1)}, u32[]{:S(2)}, u32[]{:S(2)}) collective-permute-start(bf16[1280,128]{1,0:T(8,128)(2,1)S(1)} %collective-permute-done.14.refs_0_), channel_id=1, source_target_pairs={{0,1},{1,0},{2,3},{3,2},{4,5},{5,4},{6,7},{7,6},{8,9},{9,8},{10,11... | collective-permute-start | bytes 983048 | tf_op jit(solution)/shard_map/ppermute | solution.py:288
